TPU v7x, 32 devices: a whole 2x2x4 slice. The times are simulated.
32 devices in a mesh: grp: 4 (over y, x), mem: 8 (over z, core).
Axes of the slice: x: 2, y: 2, z: 4, core: 2. Of those that a mesh axis runs over, the one named last changes fastest.
Arguments:
- embeddings: bfloat16 [4096, 1024], P(('grp', 'mem')), may hold values from -6 to 6
- cluster: int32 [4096, 1], P(('grp', 'mem')), may hold values from 0 to 3; in each aligned block of 128 rows (0 to 127, 128 to 255, ...) at most 64 rows name the same one
- rank: int32 [4096], P(('grp', 'mem')), may hold values from 0 to 1048575
Outputs:
- similarity: float32 [4096], P(('grp', 'mem'))
Inputs may be any that keep to these rules, and one draw needn't show every extreme that they name: `cluster`: in each aligned block of 128 rows (the rows of one device) no group is named by more than 64 rows. A smaller rank is earlier; equal ranks are not earlier.
All inputs are finite; a program needn't handle non-finite values.
Results may differ from a plain program's by a relative error of at most 0.0013.
Values may be sent and summed in bfloat16 or wider, within the bound.
No kernel may reach another device: no remote copies, remote signals or barrier semaphores. Data moves between devices by JAX's collectives and lax.ppermute only.
A program may use at most 64 MiB of HBM per device.

v0:
```python
import jax
import jax.numpy as jnp
from jax import lax
from jax.sharding import PartitionSpec as P

absent_rank = 1073741824


def from_partner(block, axis, distance):
    count = lax.axis_size(axis)
    route = []
    for low in range(count):
        high = low | 1 << distance
        if high != low and high < count:
            route += [(low, high), (high, low)]
    return lax.ppermute(block, axis, route)


def block_gram(queries, others):
    return lax.dot_general(
        queries, others, (((1,), (1,)), ((), ())), preferred_element_type=jnp.float32
    )


def row_maxima(gram, query_rank, other_rank):
    earlier = other_rank[None, :] < query_rank[:, None]
    return jnp.max(jnp.where(earlier, gram, jnp.float32(-1.0)), axis=1)


def body(embeddings, cluster, rank):
    rows = embeddings.shape[0]
    width = embeddings.shape[1]
    groups = lax.axis_size("grp")
    capacity = max(2, 2 * rows // groups)
    slots = groups * capacity
    wide = embeddings.astype(jnp.float32)
    normed = (wide * lax.rsqrt(jnp.sum(wide * wide, axis=1, keepdims=True) + 1e-06)).astype(
        jnp.bfloat16
    )
    owner = cluster[:, 0]
    onehot = (owner[:, None] == jnp.arange(groups, dtype=jnp.int32)[None, :]).astype(jnp.int32)
    before = jnp.cumsum(onehot, axis=0) - onehot
    position = jnp.sum(before * onehot, axis=1)
    slot = owner * capacity + position
    outgoing = jnp.zeros((slots, width), jnp.bfloat16).at[slot].set(normed)
    out_rank = jnp.full((slots,), absent_rank, jnp.int32).at[slot].set(rank)
    keys, key_rank = (
        lax.all_to_all(outgoing, "grp", split_axis=0, concat_axis=0, tiled=True),
        lax.all_to_all(out_rank, "grp", split_axis=0, concat_axis=0, tiled=True),
    )
    members = lax.axis_size("mem")
    levels = members.bit_length() - 1
    low_bits = levels // 2
    member = lax.axis_index("mem")
    query_block, query_rank = (keys, key_rank)
    for level in range(low_bits):
        upper = member // (1 << level) % 2 == 1
        got_rows, got_rank = from_partner((query_block, query_rank), "mem", level)
        query_block = jnp.where(
            upper,
            jnp.concatenate([got_rows, query_block], 0),
            jnp.concatenate([query_block, got_rows], 0),
        )
        query_rank = jnp.where(
            upper,
            jnp.concatenate([got_rank, query_rank], 0),
            jnp.concatenate([query_rank, got_rank], 0),
        )
    key_block, key_ranks = (keys, key_rank)
    for level in range(low_bits, levels):
        got_rows, got_rank = from_partner((key_block, key_ranks), "mem", level)
        key_block = jnp.concatenate([key_block, got_rows], 0)
        key_ranks = jnp.concatenate([key_ranks, got_rank], 0)
    partial_value = row_maxima(block_gram(query_block, key_block), query_rank, key_ranks)
    for level in reversed(range(low_bits)):
        upper = member // (1 << level) % 2 == 1
        half = partial_value.shape[0] // 2
        lower_part = partial_value[:half]
        upper_part = partial_value[half:]
        kept = jnp.where(upper, upper_part, lower_part)
        sent = jnp.where(upper, lower_part, upper_part)
        received = from_partner(sent, "mem", level)
        partial_value = jnp.maximum(kept, received)
    home = lax.all_to_all(partial_value, "grp", split_axis=0, concat_axis=0, tiled=True)
    return home[slot]


def solution(mesh):
    in_specs = (P(("grp", "mem"), None), P(("grp", "mem"), None), P(("grp", "mem")))
    out_specs = P(("grp", "mem"))
    return jax.shard_map(body, mesh=mesh, in_specs=in_specs, out_specs=out_specs, check_vma=False)
```

profile of v0, /device:TPU:0, one launch (start us, length us, event | category | flops | bytes accessed | tf_op | source)
XLA Modules:
  0.0 92.4 jit_solution(112546329258295398)
XLA Ops:
  0.0 0.7 fusion.23
  0.7 0.2 reduce_window_sum.11
  0.9 0.8 select_reduce_fusion.1
  1.7 0.7 fusion.25
  2.4 1.1 %fusion.17 = f32[128]{0:T(128)S(1)} fusion(bf16[128,1024]{1,0:T(8,128)(2,1)} %param.3), kind=kLoop, calls=%fused_computation.20 | loop fusion | flops 393088 | bytes 262656 | tf_op jit(solution)/shard_map/reduce_sum | solution.py:37
  3.5 1.8 %scatter_custom_fusion.1 = bf16[256,1024]{1,0:T(8,128)(2,1)S(1)} fusion(s32[128]{0:T(128)S(1)} %fusion.25, bf16[128,1024]{1,0:T(8,128)(2,1)} %param.3, f32[128]{0:T(128)S(1)} %add_rsqrt_fusion, bf16[]{:T(256)} %constant.49.clone.1), kind=kCustom, calls=%fused_computation.22 | custom fusion | flops 393216 | bytes 786946 | tf_op jit(solution)/shard_map/scatter | solution.py:45
  5.3 13.5 %all_to_all.36 = bf16[4,64,1024]{2,1,0:T(8,128)(2,1)S(1)} all-to-all(bf16[4,64,1024]{2,1,0:T(8,128)(2,1)S(1)} %bitcast.13), channel_id=1, replica_groups=mesh['grp'=4,'mem'=8] {'grp'}, dimensions={0} | all-to-all | bytes 1048576 | tf_op jit(solution)/shard_map/all_to_all | solution.py:48
  18.8 1.6 %collective-permute-start.4 = (bf16[256,1024]{1,0:T(8,128)(2,1)S(1)}, bf16[256,1024]{1,0:T(8,128)(2,1)S(1)}, u32[]{:S(2)}, u32[]{:S(2)}) collective-permute-start(bf16[256,1024]{1,0:T(8,128)(2,1)S(1)} %bitcast.14), channel_id=1, source_target_pairs={{0,2},{2,0},{1,3},{3,1},{4,6},{6,4},{5,7},{7,5},{8,10},{10,8},{9,1... | collective-permute-start | bytes 1572872 | tf_op jit(solution)/shard_map/ppermute | solution.py:16
  20.4 10.6 %collective-permute-done.4 = bf16[256,1024]{1,0:T(8,128)(2,1)S(1)} collective-permute-done((bf16[256,1024]{1,0:T(8,128)(2,1)S(1)}, bf16[256,1024]{1,0:T(8,128)(2,1)S(1)}, u32[]{:S(2)}, u32[]{:S(2)}) %collective-permute-start.4) | collective-permute-done | bytes 524320 | tf_op jit(solution)/shard_map/ppermute | solution.py:16
  31.0 0.1 pad_maximum_fusion
  31.1 2.7 %collective-permute-start.5 = (bf16[512,1024]{1,0:T(8,128)(2,1)S(1)}, bf16[512,1024]{1,0:T(8,128)(2,1)S(1)}, u32[]{:S(2)}, u32[]{:S(2)}) collective-permute-start(bf16[512,1024]{1,0:T(8,128)(2,1)S(1)} %pad_maximum_fusion), channel_id=1, source_target_pairs={{0,4},{4,0},{1,5},{5,1},{2,6},{6,2},{3,7},{7,3},{8,12},{12,8},{9,1... | collective-permute-start | bytes 3145736 | tf_op jit(solution)/shard_map/ppermute | solution.py:16
  33.7 1.1 %scatter_custom_fusion = s32[256]{0:T(256)S(1)} fusion(s32[128]{0:T(128)S(1)} %fusion.25, s32[128]{0:T(128)} %param.5, s32[]{:T(128)} %constant.46.clone.1), kind=kCustom, calls=%fused_computation.39 | custom fusion | bytes 1536 | tf_op jit(solution)/shard_map/scatter | solution.py:46
  34.8 0.1 all_to_all.24
  34.9 7.0 %all_to_all.37 = s32[4,64,1]{1,2,0:T(1,128)S(1)} all-to-all(s32[4,64,1]{1,2,0:T(1,128)S(1)} %bitcast.18), channel_id=1, replica_groups=mesh['grp'=4,'mem'=8] {'grp'}, dimensions={0} | all-to-all | bytes 2048 | tf_op jit(solution)/shard_map/all_to_all | solution.py:49
  41.9 0.5 broadcast.40
  42.4 0.7 reduce.6
  43.1 0.1 all_to_all.26
  43.2 1.6 %collective-permute-start = (s32[256]{0:T(256)S(1)}, s32[256]{0:T(256)S(1)}, u32[]{:S(2)}, u32[]{:S(2)}) collective-permute-start(s32[256]{0:T(256)S(1)} %all_to_all.26), channel_id=1, source_target_pairs={{0,2},{2,0},{1,3},{3,1},{4,6},{6,4},{5,7},{7,5},{8,10},{10,8},{9,1... | collective-permute-start | bytes 3080 | tf_op jit(solution)/shard_map/ppermute | solution.py:16
  44.8 0.0 collective-permute-done.2
  44.8 9.1 %collective-permute-done = s32[256]{0:T(256)S(1)} collective-permute-done((s32[256]{0:T(256)S(1)}, s32[256]{0:T(256)S(1)}, u32[]{:S(2)}, u32[]{:S(2)}) %collective-permute-start) | collective-permute-done | bytes 1056 | tf_op jit(solution)/shard_map/ppermute | solution.py:16
  53.9 2.3 %collective-permute-start.1 = (s32[512]{0:T(512)S(1)}, s32[512]{0:T(512)S(1)}, u32[]{:S(2)}, u32[]{:S(2)}) collective-permute-start(s32[512]{0:T(512)S(1)} %get-tuple-element.6), channel_id=1, source_target_pairs={{0,4},{4,0},{1,5},{5,1},{2,6},{6,2},{3,7},{7,3},{8,12},{12,8},{9,1... | collective-permute-start | bytes 6152 | tf_op jit(solution)/shard_map/ppermute | solution.py:16
  56.2 20.9 %collective-permute-done.1 = s32[512]{0:T(512)S(1)} collective-permute-done((s32[512]{0:T(512)S(1)}, s32[512]{0:T(512)S(1)}, u32[]{:S(2)}, u32[]{:S(2)}) %collective-permute-start.1) | collective-permute-done | bytes 2080 | tf_op jit(solution)/shard_map/ppermute | solution.py:16
  77.2 2.6 %select_reduce_fusion = f32[512]{0:T(512)S(1)} fusion(bf16[512,1024]{1,0:T(8,128)(2,1)S(1)} %collective-permute-done.5, bf16[256,1024]{1,0:T(8,128)(2,1)S(1)} %collective-permute-done.4, bf16[256,1024]{1,0:T(8,128)(2,1)S(1)} %bitcast.17, bf16[256,1024]{1,0:T(8,128)(2,1)} %collective-permute-done.3, s32[1024]{0:T(1024)S(1)} %pad_add_fusion, ...), kind=kOutput, calls=%fused_computation.9 | convolution fusion | flops 1086324224 | bytes 2629633 | tf_op jit(solution)/shard_map/dot_general | solution.py:20
  79.8 0.1 collective-permute-start.6
  79.8 1.1 %collective-permute-done.6 = f32[256]{0:T(256)S(1)} collective-permute-done((f32[256]{0:T(256)S(1)}, f32[256]{0:T(256)S(1)}, u32[]{:S(2)}, u32[]{:S(2)}) %collective-permute-start.6) | collective-permute-done | bytes 1056 | tf_op jit(solution)/shard_map/ppermute | solution.py:16
  81.0 0.7 all_to_all.30
  81.7 3.2 %all-to-all-start.2 = ((f32[4,64,1]{1,2,0:T(1,128)}), f32[4,64,1]{1,2,0:T(1,128)S(1)}, u32[]{:S(2)}, u32[]{:S(2)}) async-start(f32[4,64,1]{1,2,0:T(1,128)} %bitcast.6), calls=%async_computation.2 | async-start | bytes 4096 | tf_op jit(solution)/shard_map/all_to_all | solution.py:84
  84.9 4.5 %all-to-all-done.2 = f32[4,64,1]{1,2,0:T(1,128)S(1)} async-done(((f32[4,64,1]{1,2,0:T(1,128)}), f32[4,64,1]{1,2,0:T(1,128)S(1)}, u32[]{:S(2)}, u32[]{:S(2)}) %all-to-all-start.2) | async-done | bytes 1056 | tf_op jit(solution)/shard_map/all_to_all | solution.py:84
  89.4 0.5 broadcast.41
  89.9 0.7 reduce.7
  90.6 0.1 all_to_all.32
  90.7 1.8 %gather_fusion = f32[128]{0:T(128)} fusion(f32[256]{0:T(256)S(1)} %all_to_all.32, s32[1024]{0:T(1024)S(1)} %pad_clamp_fusion), kind=kCustom, calls=%fused_computation | custom fusion | bytes 1536 | tf_op jit(solution)/shard_map/gather | solution.py:85
  (10 shorter events, 0.1 us)
Async XLA Ops:
  18.8 12.2 %collective-permute-start.4 = (bf16[256,1024]{1,0:T(8,128)(2,1)S(1)}, bf16[256,1024]{1,0:T(8,128)(2,1)S(1)}, u32[]{:S(2)}, u32[]{:S(2)}) collective-permute-start(bf16[256,1024]{1,0:T(8,128)(2,1)S(1)} %bitcast.14), channel_id=1, source_target_pairs={{0,2},{2,0},{1,3},{3,1},{4,6},{6,4},{5,7},{7,5},{8,10},{10,8},{9,1... | collective-permute-start | bytes 1572872 | tf_op jit(solution)/shard_map/ppermute | solution.py:16
  31.1 46.1 %collective-permute-start.5 = (bf16[512,1024]{1,0:T(8,128)(2,1)S(1)}, bf16[512,1024]{1,0:T(8,128)(2,1)S(1)}, u32[]{:S(2)}, u32[]{:S(2)}) collective-permute-start(bf16[512,1024]{1,0:T(8,128)(2,1)S(1)} %pad_maximum_fusion), channel_id=1, source_target_pairs={{0,4},{4,0},{1,5},{5,1},{2,6},{6,2},{3,7},{7,3},{8,12},{12,8},{9,1... | collective-permute-start | bytes 3145736 | tf_op jit(solution)/shard_map/ppermute | solution.py:16
  33.7 43.4 %collective-permute-start.3 = (bf16[256,1024]{1,0:T(8,128)(2,1)S(1)}, bf16[256,1024]{1,0:T(8,128)(2,1)}, u32[]{:S(2)}, u32[]{:S(2)}) collective-permute-start(bf16[256,1024]{1,0:T(8,128)(2,1)S(1)} %bitcast.16), channel_id=1, source_target_pairs={{0,1},{1,0},{2,3},{3,2},{4,5},{5,4},{6,7},{7,6},{8,9},{9,8},{10,11... | collective-permute-start | bytes 1572872 | tf_op jit(solution)/shard_map/ppermute | solution.py:16
  43.2 1.6 %collective-permute-start.2 = (s32[256]{0:T(256)S(1)}, s32[256]{0:T(256)S(1)}, u32[]{:S(2)}, u32[]{:S(2)}) collective-permute-start(s32[256]{0:T(256)S(1)} %all_to_all.26), channel_id=1, source_target_pairs={{0,1},{1,0},{2,3},{3,2},{4,5},{5,4},{6,7},{7,6},{8,9},{9,8},{10,11... | collective-permute-start | bytes 3080 | tf_op jit(solution)/shard_map/ppermute | solution.py:16
  43.2 10.7 %collective-permute-start = (s32[256]{0:T(256)S(1)}, s32[256]{0:T(256)S(1)}, u32[]{:S(2)}, u32[]{:S(2)}) collective-permute-start(s32[256]{0:T(256)S(1)} %all_to_all.26), channel_id=1, source_target_pairs={{0,2},{2,0},{1,3},{3,1},{4,6},{6,4},{5,7},{7,5},{8,10},{10,8},{9,1... | collective-permute-start | bytes 3080 | tf_op jit(solution)/shard_map/ppermute | solution.py:16
  53.9 23.2 %collective-permute-start.1 = (s32[512]{0:T(512)S(1)}, s32[512]{0:T(512)S(1)}, u32[]{:S(2)}, u32[]{:S(2)}) collective-permute-start(s32[512]{0:T(512)S(1)} %get-tuple-element.6), channel_id=1, source_target_pairs={{0,4},{4,0},{1,5},{5,1},{2,6},{6,2},{3,7},{7,3},{8,12},{12,8},{9,1... | collective-permute-start | bytes 6152 | tf_op jit(solution)/shard_map/ppermute | solution.py:16
  79.8 1.2 %collective-permute-start.6 = (f32[256]{0:T(256)S(1)}, f32[256]{0:T(256)S(1)}, u32[]{:S(2)}, u32[]{:S(2)}) collective-permute-start(f32[256]{0:T(256)S(1)} %broadcast_select_fusion), channel_id=1, source_target_pairs={{0,1},{1,0},{2,3},{3,2},{4,5},{5,4},{6,7},{7,6},{8,9},{9,8},{10,11... | collective-permute-start | bytes 3080 | tf_op jit(solution)/shard_map/ppermute | solution.py:16
  81.7 7.7 %all-to-all-start.2 = ((f32[4,64,1]{1,2,0:T(1,128)}), f32[4,64,1]{1,2,0:T(1,128)S(1)}, u32[]{:S(2)}, u32[]{:S(2)}) async-start(f32[4,64,1]{1,2,0:T(1,128)} %bitcast.6), calls=%async_computation.2 | async-start | bytes 4096 | tf_op jit(solution)/shard_map/all_to_all | solution.py:84
where the time goes:
time: 92.8 us; the launch traced here: 92.4 us
  waiting for transfers between devices  46.2 us (50%)
  blocking collectives  20.5 us (22%)
  starting transfers between devices  11.5 us (12%)
  other arithmetic  6.71 us (7%)
  local copies, waits for them, and re-layouts  4.82 us (5%)
  matrix products  2.57 us (3%)
    ppermute x7, waiting for transfers between devices, from_partner(): return lax.ppermute(block, axis, route)  41.7 us
    all_to_all x1, blocking collectives, body(): lax.all_to_all(outgoing, 'grp', split_axis=0, concat_axis=0, tiled=True)  13.5 us
    ppermute x7, starting transfers between devices, from_partner(): return lax.ppermute(block, axis, route)  8.28 us
    all_to_all x1, blocking collectives, body(): lax.all_to_all(out_rank, 'grp', split_axis=0, concat_axis=0, tiled=True)  7 us
    all_to_all x1, waiting for transfers between devices, body(): lax.all_to_all(partial_value, 'grp', split_axis=0, concat_axis=0, tiled=T...  4.48 us
    all_to_all x1, starting transfers between devices, body(): lax.all_to_all(partial_value, 'grp', split_axis=0, concat_axis=0, tiled=T...  3.24 us
    dot_general x1, matrix products, block_gram(): lax.dot_general(queries, others, (((1,), (1,)), ((), ())), preferred_elem...  2.57 us
  transfers between devices with their start and end apart: 8, of which 5 were waited for; matrix products, arithmetic and copies ran while one was open for 2% of the time, Pallas kernels for 0%

commit v1 on v0

v1 whole, which is shorter than its diff:
```python
import functools

import jax
import jax.numpy as jnp
from jax import lax
from jax.experimental import pallas as pl
from jax.experimental.pallas import tpu as pltpu
from jax.sharding import PartitionSpec as P


META = 8
QUERIES = 8
SHIFT = 21


def meeting_slots(count):
    slots = []
    for distance in range(1, (count + 1) // 2):
        slots.append([(i, (i + distance) % count) for i in range(count)])
    if count % 2 == 0:
        half = count // 2
        slots.append([(i, i + half) if i % 2 == 0 else (i + half, i) for i in range(half)])
    return slots[::-1]


def prepare_kernel(x_ref, key_ref, out_ref):
    rows = x_ref.shape[0]
    wide = x_ref[...].astype(jnp.float32)
    scale = lax.rsqrt(jnp.sum(wide * wide, axis=1, keepdims=True) + 1e-06)
    out_ref[0:rows, :] = (wide * scale).astype(jnp.bfloat16)
    key = key_ref[...]
    digit = lax.broadcasted_iota(jnp.int32, (META, rows), 0)
    spread = jnp.where(
        digit == 0,
        key & 255,
        jnp.where(digit == 1, (key >> 8) & 255, jnp.where(digit == 2, key >> 16, 0)),
    )
    out_ref[rows : rows + META, :] = jnp.zeros((META, out_ref.shape[1]), jnp.bfloat16)
    out_ref[rows : rows + META, 0:rows] = spread.astype(jnp.float32).astype(jnp.bfloat16)


def keys_of(ref, rows):
    meta = ref[rows : rows + META, 0:rows].astype(jnp.float32)
    key = meta[0:1] + 256.0 * meta[1:2] + 65536.0 * meta[2:3]
    owner = jnp.where(key > 0.0, jnp.floor(meta[2:3] * (1.0 / 32.0)), -1.0)
    return key, owner


def column(row):
    size = row.shape[1]
    return jnp.broadcast_to(row, (size, size)).T


def places_of(members, pairs):
    grp = lax.axis_index("grp")
    mem = lax.axis_index("mem")
    core = mem % 2
    chip = mem // 2
    near = grp ^ (1 + core)
    other_near = grp ^ (2 - core)
    far = grp ^ 3
    row = chip * 2
    queries = [
        grp * members + row + core,
        grp * members + row + 1 - core,
        near * members + row + core,
        near * members + row + 1 - core,
        other_near * members + row + 1 - core,
        other_near * members + row + core,
        far * members + row + core,
        far * members + row + 1 - core,
    ]
    keys = [None]
    for pair in pairs:
        source = jnp.int32(-1)
        for side, table in enumerate(pair):
            for origin, target in table:
                source = jnp.where((core == side) & (chip == target), origin, source)
        for sender in (core, 1 - core):
            keys.append(jnp.where(source < 0, -1, grp * members + source * 2 + sender))
    return queries, keys


def similarity_kernel(groups, n_query, n_key, has_before, members, pairs, *refs):
    queries = dict(zip(n_query, refs))
    keys = dict(zip(n_key, refs[len(n_query) :]))
    out_ref = refs[-1]
    rows = refs[0].shape[0] - META
    query_places, key_places = places_of(members, pairs)
    slot_of = lax.broadcasted_iota(jnp.int32, out_ref.shape, 0)
    result = refs[-2][...] if has_before else jnp.full(out_ref.shape, -1.0, jnp.float32)
    query_keys = {j: keys_of(q, rows) for j, q in queries.items()}
    other_keys = {i: [column(v) for v in keys_of(k, rows)] for i, k in keys.items()}
    best = {}
    back = {}
    for query_list, key_list in groups:
        other_rows = jnp.concatenate([keys[i][0:rows, :] for i in key_list], axis=0)
        for start in range(0, len(query_list), 2):
            some = query_list[start : start + 2]
            query_rows = jnp.concatenate([queries[j][0:rows, :] for j in some], axis=0)
            gram = lax.dot_general(
                other_rows,
                query_rows,
                (((1,), (1,)), ((), ())),
                preferred_element_type=jnp.float32,
            )
            for a, i in enumerate(key_list):
                key, owner = other_keys[i]
                for b, j in enumerate(some):
                    query_key, query_owner = query_keys[j]
                    tile = gram[a * rows : (a + 1) * rows, b * rows : (b + 1) * rows]
                    same = owner == query_owner
                    found = jnp.where(same & (key < query_key), tile, -1.0)
                    best[j] = jnp.maximum(best[j], found) if j in best else found
                    if key_places[i] is not None:
                        found = jnp.where(same & (query_key < key), tile, -1.0)
                        back[i] = jnp.maximum(back[i], found) if i in back else found
    maxima = [(query_places[j], value) for j, value in best.items()]
    maxima += [(key_places[i], value.T) for i, value in back.items()]
    for place, value in maxima:
        result = jnp.maximum(
            result,
            jnp.where(slot_of == place, jnp.max(value, axis=0, keepdims=True), -1.0),
        )
    out_ref[...] = result


def body(embeddings, cluster, rank):
    rows, width = embeddings.shape
    groups = lax.axis_size("grp")
    members = lax.axis_size("mem")
    chips = members // 2
    devices = groups * members
    vmem = pl.BlockSpec(memory_space=pltpu.VMEM)
    key = cluster[:, 0] * (1 << SHIFT) + rank + 1
    block = pl.pallas_call(
        prepare_kernel,
        out_shape=jax.ShapeDtypeStruct((rows + META, width), jnp.bfloat16),
        in_specs=[vmem] * 2,
        out_specs=vmem,
        compiler_params=pltpu.CompilerParams(vmem_limit_bytes=4 << 20),
        name="prepare",
    )(embeddings, key.reshape(1, rows))

    def send(value, route):
        return lax.ppermute(value, ("grp", "mem"), route)

    def swap(value):
        return send(value, [(i, i ^ 1) for i in range(devices)])

    def across(step):
        return [
            (g * members + m, (g ^ step[m % 2]) * members + m)
            for g in range(groups)
            for m in range(members)
        ]

    def along(pair):
        return [
            (g * members + 2 * a + c, g * members + 2 * b + c)
            for g in range(groups)
            for c, slot in enumerate(pair)
            for a, b in slot
        ]

    slots = meeting_slots(chips)
    slots += [[]] * (len(slots) % 2)
    pairs = [slots[i : i + 2] for i in range(0, len(slots), 2)]
    partner = swap(block)
    near = send(block, across((1, 2)))
    near_partner = send(partner, across((1, 2)))
    far = send(near, across((2, 1)))
    keys = [block]
    for pair in pairs:
        keys.append(send(block, along(pair)))
        keys.append(send(partner, along(pair)))
    queries = [
        block,
        partner,
        near,
        near_partner,
        swap(near),
        swap(near_partner),
        far,
        swap(far),
    ]

    def maxima(work, before):
        used_queries = sorted({j for some, _ in work for j in some})
        used_keys = sorted({i for _, some in work for i in some})
        operands = [queries[j] for j in used_queries] + [keys[i] for i in used_keys]
        operands += [] if before is None else [before]
        products = sum(len(some) * len(other) for some, other in work)
        return pl.pallas_call(
            functools.partial(
                similarity_kernel,
                work,
                used_queries,
                used_keys,
                before is not None,
                members,
                pairs,
            ),
            out_shape=jax.ShapeDtypeStruct((devices, rows), jnp.float32),
            in_specs=[vmem] * len(operands),
            out_specs=vmem,
            compiler_params=pltpu.CompilerParams(vmem_limit_bytes=16 << 20),
            cost_estimate=pl.CostEstimate(
                flops=2 * products * rows * rows * width,
                bytes_accessed=0,
                transcendentals=0,
            ),
        )(*operands)

    last = len(keys) - 1
    near_queries = list(range(QUERIES - 2))
    first = list(range(last))
    found = maxima([(near_queries, first)], None)
    found = maxima([([QUERIES - 2, QUERIES - 1], first)], found)
    found = maxima([(list(range(QUERIES)), [last])], found)
    home = lax.all_to_all(
        found, ("grp", "mem"), split_axis=0, concat_axis=0, tiled=True
    )
    return jnp.max(home, axis=0)


def solution(mesh):
    in_specs = (P(("grp", "mem"), None), P(("grp", "mem"), None), P(("grp", "mem")))
    out_specs = P(("grp", "mem"))
    return jax.shard_map(
        body, mesh=mesh, in_specs=in_specs, out_specs=out_specs, check_vma=False
    )
```

time: 92.8 us -> 41 us (0.44)
  waiting for transfers between devices: 46.2 us -> 7.41 us
  blocking collectives: 20.5 us -> 12.7 us
  other arithmetic: 6.71 us -> 1.23 us
  starting transfers between devices: 11.5 us -> 16.1 us
  local copies, waits for them, and re-layouts: 4.82 us -> 0.95 us
  matrix products: 2.57 us -> 0 us
  Pallas kernels: 0 us -> 2.27 us
    ppermute x7 -> x9, waiting for transfers between devices: 41.7 us -> 7.41 us  [send(): return lax.ppermute(value, ('grp', 'mem'), route)]
    ppermute x7 -> x9, starting transfers between devices: 8.28 us -> 16.1 us  [send(): return lax.ppermute(value, ('grp', 'mem'), route)]
    all_to_all x2 -> x1, blocking collectives: 20.5 us -> 12.7 us  [body(): lax.all_to_all(found, ('grp', 'mem'), split_axis=0, concat_axis=0, tiled=...]
    all_to_all x1 -> x0, waiting for transfers between devices: 4.48 us -> none  [body(): lax.all_to_all(partial_value, 'grp', split_axis=0, concat_axis=0, tiled=T...]
    all_to_all x1 -> x0, starting transfers between devices: 3.24 us -> none  [body(): lax.all_to_all(partial_value, 'grp', split_axis=0, concat_axis=0, tiled=T...]
    dot_general x1 -> x0, matrix products: 2.57 us -> none  [block_gram(): lax.dot_general(queries, others, (((1,), (1,)), ((), ())), preferred_elem...]
    pallas_call x0 -> x4, Pallas kernels: none -> 2.27 us  [the longest x3 2.13 us: maxima(): pl.pallas_call(functools.partial(similarity_kernel, work, used_queries, u...]
    all_to_all x6 -> x0, local copies, waits for them, and re-layouts: 1.95 us -> none  [the longest x3 1.27 us: body(): lax.all_to_all(partial_value, 'grp', split_axis=0, concat_axis=0, tiled=T...]
  transfers between devices with their start and end apart: 8 -> 9, of which waited for: 5 -> 2; matrix products, arithmetic and copies ran while one was open for 2% -> 0% of each run, Pallas kernels for 0% -> 3%
where the time goes in v1:
time: 41 us; the launch traced here: 40.8 us
  starting transfers between devices  16.1 us (39%)
  blocking collectives  12.7 us (31%)
  waiting for transfers between devices  7.41 us (18%)
  Pallas kernels  2.27 us (6%)
  other arithmetic  1.23 us (3%)
  local copies, waits for them, and re-layouts  0.95 us (2%)
    ppermute x9, starting transfers between devices, send(): return lax.ppermute(value, ('grp', 'mem'), route)  16.1 us
    all_to_all x1, blocking collectives, body(): lax.all_to_all(found, ('grp', 'mem'), split_axis=0, concat_axis=0, tiled=...  12.7 us
    ppermute x9, waiting for transfers between devices, send(): return lax.ppermute(value, ('grp', 'mem'), route)  7.41 us
    pallas_call x3, Pallas kernels, maxima(): pl.pallas_call(functools.partial(similarity_kernel, work, used_queries, u...  2.13 us
    unnamed x2, local copies, waits for them, and re-layouts  0.95 us
  transfers between devices with their start and end apart: 9, of which 2 were waited for; matrix products, arithmetic and copies ran while one was open for 0% of the time, Pallas kernels for 3%

profile of v1, /device:TPU:0, one launch (start us, length us, event | category | flops | bytes accessed | tf_op | source)
XLA Modules:
  0.0 40.8 jit_solution(17660844534452924271)
XLA Ops:
  0.0 0.7 %fusion.1.key_ref = s32[1,128]{1,0:T(1,128)S(1)} fusion(s32[128]{0:T(128)} %param.5, s32[128,1]{0,1:T(1,128)} %param.4), kind=kLoop, calls=%fused_computation.2 | loop fusion | flops 384 | bytes 1536 | tf_op jit(solution)/shard_map/reshape | solution.py:143
  0.7 0.0 copy-start
  0.7 0.9 %copy-done = bf16[128,1024]{1,0:T(8,128)(2,1)S(1)} copy-done((bf16[128,1024]{1,0:T(8,128)(2,1)S(1)}, bf16[128,1024]{1,0:T(8,128)(2,1)}, u32[]{:S(2)}) %copy-start) | copy-done | bytes 262168
  1.6 0.1 prepare.1.refs_0_.refs_6_.refs_2_
  1.8 0.6 %collective-permute-start = (bf16[136,1024]{1,0:T(8,128)(2,1)S(1)}, bf16[136,1024]{1,0:T(8,128)(2,1)S(1)}, u32[]{:S(2)}, u32[]{:S(2)}) collective-permute-start(bf16[136,1024]{1,0:T(8,128)(2,1)S(1)} %prepare.1.refs_0_.refs_6_.refs_2_), channel_id=1, source_target_pairs={{0,1},{1,0},{2,3},{3,2},{4,5},{5,4},{6,7},{7,6},{8,9},{9,8},{10,11... | collective-permute-start | bytes 835592 | tf_op jit(solution)/shard_map/ppermute | solution.py:146
  2.3 2.6 %collective-permute-start.1 = (bf16[136,1024]{1,0:T(8,128)(2,1)S(1)}, bf16[136,1024]{1,0:T(8,128)(2,1)S(1)}, u32[]{:S(2)}, u32[]{:S(2)}) collective-permute-start(bf16[136,1024]{1,0:T(8,128)(2,1)S(1)} %prepare.1.refs_0_.refs_6_.refs_2_), channel_id=1, source_target_pairs={{0,8},{1,17},{2,10},{3,19},{4,12},{5,21},{6,14},{7,23},{8,0},{9,25... | collective-permute-start | bytes 835592 | tf_op jit(solution)/shard_map/ppermute | solution.py:146
  4.9 0.0 collective-permute-done.refs_1_
  4.9 1.5 %collective-permute-start.2 = (bf16[136,1024]{1,0:T(8,128)(2,1)S(1)}, bf16[136,1024]{1,0:T(8,128)(2,1)S(1)}, u32[]{:S(2)}, u32[]{:S(2)}) collective-permute-start(bf16[136,1024]{1,0:T(8,128)(2,1)S(1)} %collective-permute-done.refs_1_), channel_id=1, source_target_pairs={{0,8},{1,17},{2,10},{3,19},{4,12},{5,21},{6,14},{7,23},{8,0},{9,25... | collective-permute-start | bytes 835592 | tf_op jit(solution)/shard_map/ppermute | solution.py:146
  6.4 3.0 %collective-permute-done.1.refs_2_ = bf16[136,1024]{1,0:T(8,128)(2,1)S(1)} collective-permute-done((bf16[136,1024]{1,0:T(8,128)(2,1)S(1)}, bf16[136,1024]{1,0:T(8,128)(2,1)S(1)}, u32[]{:S(2)}, u32[]{:S(2)}) %collective-permute-start.1) | collective-permute-done | bytes 278560 | tf_op jit(solution)/shard_map/ppermute | solution.py:146
  9.4 2.0 %collective-permute-start.5 = (bf16[136,1024]{1,0:T(8,128)(2,1)S(1)}, bf16[136,1024]{1,0:T(8,128)(2,1)S(1)}, u32[]{:S(2)}, u32[]{:S(2)}) collective-permute-start(bf16[136,1024]{1,0:T(8,128)(2,1)S(1)} %collective-permute-done.1.refs_2_), channel_id=1, source_target_pairs={{0,16},{1,9},{2,18},{3,11},{4,20},{5,13},{6,22},{7,15},{8,24},{9,1... | collective-permute-start | bytes 835592 | tf_op jit(solution)/shard_map/ppermute | solution.py:146
  11.5 4.5 %collective-permute-start.8 = (bf16[136,1024]{1,0:T(8,128)(2,1)S(1)}, bf16[136,1024]{1,0:T(8,128)(2,1)S(1)}, u32[]{:S(2)}, u32[]{:S(2)}) collective-permute-start(bf16[136,1024]{1,0:T(8,128)(2,1)S(1)} %prepare.1.refs_0_.refs_6_.refs_2_), channel_id=1, source_target_pairs={{0,4},{6,2},{1,3},{3,5},{5,7},{7,1},{8,12},{14,10},{9,11},{11,13},... | collective-permute-start | bytes 835592 | tf_op jit(solution)/shard_map/ppermute | solution.py:146
  16.0 0.1 collective-permute-start.3
  16.0 0.0 collective-permute-done.2.refs_3_
  16.1 0.5 %collective-permute-start.4 = (bf16[136,1024]{1,0:T(8,128)(2,1)S(1)}, bf16[136,1024]{1,0:T(8,128)(2,1)S(1)}, u32[]{:S(2)}, u32[]{:S(2)}) collective-permute-start(bf16[136,1024]{1,0:T(8,128)(2,1)S(1)} %collective-permute-done.2.refs_3_), channel_id=1, source_target_pairs={{0,1},{1,0},{2,3},{3,2},{4,5},{5,4},{6,7},{7,6},{8,9},{9,8},{10,11... | collective-permute-start | bytes 835592 | tf_op jit(solution)/shard_map/ppermute | solution.py:146
  16.5 0.0 collective-permute-done.5.refs_0_.refs_6_
  16.5 0.1 collective-permute-start.6
  16.6 4.4 %collective-permute-start.7 = (bf16[136,1024]{1,0:T(8,128)(2,1)S(1)}, bf16[136,1024]{1,0:T(8,128)(2,1)S(1)}, u32[]{:S(2)}, u32[]{:S(2)}) collective-permute-start(bf16[136,1024]{1,0:T(8,128)(2,1)S(1)} %collective-permute-done.refs_1_), channel_id=1, source_target_pairs={{0,4},{6,2},{1,3},{3,5},{5,7},{7,1},{8,12},{14,10},{9,11},{11,13},... | collective-permute-start | bytes 835592 | tf_op jit(solution)/shard_map/ppermute | solution.py:146
  21.0 0.0 collective-permute-done.8.refs_7_.refs_3_
  21.0 0.0 collective-permute-done.3.refs_4_
  21.0 0.0 collective-permute-done.4.refs_5_
  21.0 0.8 %shard_map.37.refs_4_ = f32[32,128]{1,0:T(8,128)S(1)} custom-call(bf16[136,1024]{1,0:T(8,128)(2,1)S(1)} %prepare.1.refs_0_.refs_6_.refs_2_, bf16[136,1024]{1,0:T(8,128)(2,1)S(1)} %collective-permute-done.refs_1_, bf16[136,1024]{1,0:T(8,128)(2,1)S(1)} %collective-permute-done.1.refs_2_, bf16[136,1024]{1,0:T(8,128)(2,1)S(1)} %collective-permute-done.2.refs_3_, ...), custom_call_target="tpu_custom_call" | custom-call | flops 402653184 | tf_op jit(solution)/shard_map/pallas_call | solution.py:194
  21.8 0.0 collective-permute-done.6.refs_1_.refs_7_
  21.8 0.4 %shard_map.38.refs_9_ = f32[32,128]{1,0:T(8,128)S(1)} custom-call(bf16[136,1024]{1,0:T(8,128)(2,1)S(1)} %collective-permute-done.5.refs_0_.refs_6_, bf16[136,1024]{1,0:T(8,128)(2,1)S(1)} %collective-permute-done.6.refs_1_.refs_7_, bf16[136,1024]{1,0:T(8,128)(2,1)S(1)} %prepare.1.refs_0_.refs_6_.refs_2_, ...), custom_call_target="tpu_custom_call" | custom-call | flops 134217728 | tf_op jit(solution)/shard_map/pallas_call | solution.py:194
  22.2 4.3 %collective-permute-done.7.refs_8_ = bf16[136,1024]{1,0:T(8,128)(2,1)S(1)} collective-permute-done((bf16[136,1024]{1,0:T(8,128)(2,1)S(1)}, bf16[136,1024]{1,0:T(8,128)(2,1)S(1)}, u32[]{:S(2)}, u32[]{:S(2)}) %collective-permute-start.7) | collective-permute-done | bytes 278560 | tf_op jit(solution)/shard_map/ppermute | solution.py:146
  26.6 1.0 %shard_map.39 = f32[32,128]{1,0:T(8,128)S(1)} custom-call(bf16[136,1024]{1,0:T(8,128)(2,1)S(1)} %prepare.1.refs_0_.refs_6_.refs_2_, bf16[136,1024]{1,0:T(8,128)(2,1)S(1)} %collective-permute-done.refs_1_, bf16[136,1024]{1,0:T(8,128)(2,1)S(1)} %collective-permute-done.1.refs_2_, bf16[136,1024]{1,0:T(8,128)(2,1)S(1)} %collective-permute-done.2.refs_3_, ...), custom_call_target="tpu_custom_call" | custom-call | flops 268435456 | tf_op jit(solution)/shard_map/pallas_call | solution.py:194
  27.5 12.7 %all_to_all.9 = f32[32,1,128]{2,1,0:T(1,128)S(1)} all-to-all(f32[32,1,128]{2,1,0:T(1,128)S(1)} %bitcast.11), channel_id=1, replica_groups=mesh['grp'=4,'mem'=8] {'grp','mem'}, dimensions={0} | all-to-all | bytes 32768 | tf_op jit(solution)/shard_map/all_to_all | solution.py:221
  40.2 0.6 %reduce_max.9 = f32[128]{0:T(128)} reduce(f32[32,1,128]{2,1,0:T(1,128)S(1)} %all_to_all.9, f32[]{:T(128)} %constant.2.clone.1), dimensions={0,1}, to_apply=%region_0.0 | reduce | flops 3968 | bytes 16900 | tf_op jit(solution)/shard_map/reduce_max | solution.py:224
Async XLA Ops:
  0.7 0.9 %copy-start = (bf16[128,1024]{1,0:T(8,128)(2,1)S(1)}, bf16[128,1024]{1,0:T(8,128)(2,1)}, u32[]{:S(2)}) copy-start(bf16[128,1024]{1,0:T(8,128)(2,1)} %x_ref.1) | copy-start | bytes 786436
  1.8 3.1 %collective-permute-start = (bf16[136,1024]{1,0:T(8,128)(2,1)S(1)}, bf16[136,1024]{1,0:T(8,128)(2,1)S(1)}, u32[]{:S(2)}, u32[]{:S(2)}) collective-permute-start(bf16[136,1024]{1,0:T(8,128)(2,1)S(1)} %prepare.1.refs_0_.refs_6_.refs_2_), channel_id=1, source_target_pairs={{0,1},{1,0},{2,3},{3,2},{4,5},{5,4},{6,7},{7,6},{8,9},{9,8},{10,11... | collective-permute-start | bytes 835592 | tf_op jit(solution)/shard_map/ppermute | solution.py:146
  2.3 7.1 %collective-permute-start.1 = (bf16[136,1024]{1,0:T(8,128)(2,1)S(1)}, bf16[136,1024]{1,0:T(8,128)(2,1)S(1)}, u32[]{:S(2)}, u32[]{:S(2)}) collective-permute-start(bf16[136,1024]{1,0:T(8,128)(2,1)S(1)} %prepare.1.refs_0_.refs_6_.refs_2_), channel_id=1, source_target_pairs={{0,8},{1,17},{2,10},{3,19},{4,12},{5,21},{6,14},{7,23},{8,0},{9,25... | collective-permute-start | bytes 835592 | tf_op jit(solution)/shard_map/ppermute | solution.py:146
  4.9 11.2 %collective-permute-start.2 = (bf16[136,1024]{1,0:T(8,128)(2,1)S(1)}, bf16[136,1024]{1,0:T(8,128)(2,1)S(1)}, u32[]{:S(2)}, u32[]{:S(2)}) collective-permute-start(bf16[136,1024]{1,0:T(8,128)(2,1)S(1)} %collective-permute-done.refs_1_), channel_id=1, source_target_pairs={{0,8},{1,17},{2,10},{3,19},{4,12},{5,21},{6,14},{7,23},{8,0},{9,25... | collective-permute-start | bytes 835592 | tf_op jit(solution)/shard_map/ppermute | solution.py:146
  9.4 7.1 %collective-permute-start.5 = (bf16[136,1024]{1,0:T(8,128)(2,1)S(1)}, bf16[136,1024]{1,0:T(8,128)(2,1)S(1)}, u32[]{:S(2)}, u32[]{:S(2)}) collective-permute-start(bf16[136,1024]{1,0:T(8,128)(2,1)S(1)} %collective-permute-done.1.refs_2_), channel_id=1, source_target_pairs={{0,16},{1,9},{2,18},{3,11},{4,20},{5,13},{6,22},{7,15},{8,24},{9,1... | collective-permute-start | bytes 835592 | tf_op jit(solution)/shard_map/ppermute | solution.py:146
  11.5 9.5 %collective-permute-start.8 = (bf16[136,1024]{1,0:T(8,128)(2,1)S(1)}, bf16[136,1024]{1,0:T(8,128)(2,1)S(1)}, u32[]{:S(2)}, u32[]{:S(2)}) collective-permute-start(bf16[136,1024]{1,0:T(8,128)(2,1)S(1)} %prepare.1.refs_0_.refs_6_.refs_2_), channel_id=1, source_target_pairs={{0,4},{6,2},{1,3},{3,5},{5,7},{7,1},{8,12},{14,10},{9,11},{11,13},... | collective-permute-start | bytes 835592 | tf_op jit(solution)/shard_map/ppermute | solution.py:146
  16.0 5.0 %collective-permute-start.3 = (bf16[136,1024]{1,0:T(8,128)(2,1)S(1)}, bf16[136,1024]{1,0:T(8,128)(2,1)S(1)}, u32[]{:S(2)}, u32[]{:S(2)}) collective-permute-start(bf16[136,1024]{1,0:T(8,128)(2,1)S(1)} %collective-permute-done.1.refs_2_), channel_id=1, source_target_pairs={{0,1},{1,0},{2,3},{3,2},{4,5},{5,4},{6,7},{7,6},{8,9},{9,8},{10,11... | collective-permute-start | bytes 835592 | tf_op jit(solution)/shard_map/ppermute | solution.py:146
  16.1 5.0 %collective-permute-start.4 = (bf16[136,1024]{1,0:T(8,128)(2,1)S(1)}, bf16[136,1024]{1,0:T(8,128)(2,1)S(1)}, u32[]{:S(2)}, u32[]{:S(2)}) collective-permute-start(bf16[136,1024]{1,0:T(8,128)(2,1)S(1)} %collective-permute-done.2.refs_3_), channel_id=1, source_target_pairs={{0,1},{1,0},{2,3},{3,2},{4,5},{5,4},{6,7},{7,6},{8,9},{9,8},{10,11... | collective-permute-start | bytes 835592 | tf_op jit(solution)/shard_map/ppermute | solution.py:146
  16.5 5.3 %collective-permute-start.6 = (bf16[136,1024]{1,0:T(8,128)(2,1)S(1)}, bf16[136,1024]{1,0:T(8,128)(2,1)S(1)}, u32[]{:S(2)}, u32[]{:S(2)}) collective-permute-start(bf16[136,1024]{1,0:T(8,128)(2,1)S(1)} %collective-permute-done.5.refs_0_.refs_6_), channel_id=1, source_target_pairs={{0,1},{1,0},{2,3},{3,2},{4,5},{5,4},{6,7},{7,6},{8,9},{9,8},{10,11... | collective-permute-start | bytes 835592 | tf_op jit(solution)/shard_map/ppermute | solution.py:146
  16.6 9.9 %collective-permute-start.7 = (bf16[136,1024]{1,0:T(8,128)(2,1)S(1)}, bf16[136,1024]{1,0:T(8,128)(2,1)S(1)}, u32[]{:S(2)}, u32[]{:S(2)}) collective-permute-start(bf16[136,1024]{1,0:T(8,128)(2,1)S(1)} %collective-permute-done.refs_1_), channel_id=1, source_target_pairs={{0,4},{6,2},{1,3},{3,5},{5,7},{7,1},{8,12},{14,10},{9,11},{11,13},... | collective-permute-start | bytes 835592 | tf_op jit(solution)/shard_map/ppermute | solution.py:146

commit v2 on v1

--- a/solution.py
+++ b/solution.py
@@ -8,8 +8,9 @@
 from jax.sharding import PartitionSpec as P
 
 
-META = 8
+META = 16
 QUERIES = 8
+CHUNKS = 4
 SHIFT = 21
 
 
@@ -23,24 +24,52 @@
     return slots[::-1]
 
 
-def prepare_kernel(x_ref, key_ref, out_ref):
+def prepare_kernel(x_ref, cluster_ref, rank_ref, out_ref, x_buf, meta_buf, sems):
     rows = x_ref.shape[0]
-    wide = x_ref[...].astype(jnp.float32)
-    scale = lax.rsqrt(jnp.sum(wide * wide, axis=1, keepdims=True) + 1e-06)
-    out_ref[0:rows, :] = (wide * scale).astype(jnp.bfloat16)
-    key = key_ref[...]
+    part = rows // CHUNKS
+    loads = [
+        pltpu.make_async_copy(
+            x_ref.at[pl.ds(i * part, part), :],
+            x_buf.at[pl.ds(i * part, part), :],
+            sems.at[i],
+        )
+        for i in range(CHUNKS)
+    ]
+    loads.append(pltpu.make_async_copy(cluster_ref, meta_buf.at[0], sems.at[CHUNKS]))
+    loads.append(pltpu.make_async_copy(rank_ref, meta_buf.at[1], sems.at[CHUNKS + 1]))
+    for load in loads:
+        load.start()
+    width = x_ref.shape[1]
+    for i in range(CHUNKS):
+        loads[i].wait()
+        wide = x_buf[i * part : (i + 1) * part, :].astype(jnp.float32)
+        scale = lax.rsqrt(jnp.sum(wide * wide, axis=1, keepdims=True) + 1e-06)
+        narrow = (wide * scale).astype(jnp.bfloat16)
+        for start in range(0, width, rows):
+            out_ref[start + i * part : start + (i + 1) * part, :] = narrow[
+                :, start : start + rows
+            ]
+    loads[CHUNKS].wait()
+    loads[CHUNKS + 1].wait()
+    key = meta_buf[0] * (1 << SHIFT) + meta_buf[1] + 1
     digit = lax.broadcasted_iota(jnp.int32, (META, rows), 0)
     spread = jnp.where(
         digit == 0,
         key & 255,
         jnp.where(digit == 1, (key >> 8) & 255, jnp.where(digit == 2, key >> 16, 0)),
     )
-    out_ref[rows : rows + META, :] = jnp.zeros((META, out_ref.shape[1]), jnp.bfloat16)
-    out_ref[rows : rows + META, 0:rows] = spread.astype(jnp.float32).astype(jnp.bfloat16)
-
-
-def keys_of(ref, rows):
-    meta = ref[rows : rows + META, 0:rows].astype(jnp.float32)
+    out_ref[width : width + META, :] = spread.astype(jnp.float32).astype(jnp.bfloat16)
+
+
+def rows_of(ref):
+    rows = ref.shape[1]
+    return jnp.concatenate(
+        [ref[i : i + rows, :] for i in range(0, ref.shape[0] - META, rows)], axis=1
+    )
+
+
+def keys_of(ref):
+    meta = ref[ref.shape[0] - META :, :].astype(jnp.float32)
     key = meta[0:1] + 256.0 * meta[1:2] + 65536.0 * meta[2:3]
     owner = jnp.where(key > 0.0, jnp.floor(meta[2:3] * (1.0 / 32.0)), -1.0)
     return key, owner
@@ -85,19 +114,19 @@
     queries = dict(zip(n_query, refs))
     keys = dict(zip(n_key, refs[len(n_query) :]))
     out_ref = refs[-1]
-    rows = refs[0].shape[0] - META
+    rows = refs[0].shape[1]
     query_places, key_places = places_of(members, pairs)
     slot_of = lax.broadcasted_iota(jnp.int32, out_ref.shape, 0)
     result = refs[-2][...] if has_before else jnp.full(out_ref.shape, -1.0, jnp.float32)
-    query_keys = {j: keys_of(q, rows) for j, q in queries.items()}
-    other_keys = {i: [column(v) for v in keys_of(k, rows)] for i, k in keys.items()}
+    query_keys = {j: keys_of(q) for j, q in queries.items()}
+    other_keys = {i: [column(v) for v in keys_of(k)] for i, k in keys.items()}
     best = {}
     back = {}
     for query_list, key_list in groups:
-        other_rows = jnp.concatenate([keys[i][0:rows, :] for i in key_list], axis=0)
+        other_rows = jnp.concatenate([rows_of(keys[i]) for i in key_list], axis=0)
         for start in range(0, len(query_list), 2):
             some = query_list[start : start + 2]
-            query_rows = jnp.concatenate([queries[j][0:rows, :] for j in some], axis=0)
+            query_rows = jnp.concatenate([rows_of(queries[j]) for j in some], axis=0)
             gram = lax.dot_general(
                 other_rows,
                 query_rows,
@@ -132,15 +161,23 @@
     chips = members // 2
     devices = groups * members
     vmem = pl.BlockSpec(memory_space=pltpu.VMEM)
-    key = cluster[:, 0] * (1 << SHIFT) + rank + 1
+    anywhere = pl.BlockSpec(memory_space=pl.ANY)
     block = pl.pallas_call(
         prepare_kernel,
-        out_shape=jax.ShapeDtypeStruct((rows + META, width), jnp.bfloat16),
-        in_specs=[vmem] * 2,
+        out_shape=jax.ShapeDtypeStruct((width + META, rows), jnp.bfloat16),
+        in_specs=[anywhere] * 3,
         out_specs=vmem,
+        scratch_shapes=[
+            pltpu.VMEM((rows, width), jnp.bfloat16),
+            pltpu.VMEM((2, 1, rows), jnp.int32),
+            pltpu.SemaphoreType.DMA((CHUNKS + 2,)),
+        ],
         compiler_params=pltpu.CompilerParams(vmem_limit_bytes=4 << 20),
         name="prepare",
-    )(embeddings, key.reshape(1, rows))
+    )(*(
+        pltpu.with_memory_space_constraint(value, pltpu.HBM)
+        for value in (embeddings, cluster.reshape(1, rows), rank.reshape(1, rows))
+    ))
 
     def send(value, route):
         return lax.ppermute(value, ("grp", "mem"), route)
@@ -216,8 +253,9 @@
     near_queries = list(range(QUERIES - 2))
     first = list(range(last))
     found = maxima([(near_queries, first)], None)
-    found = maxima([([QUERIES - 2, QUERIES - 1], first)], found)
-    found = maxima([(list(range(QUERIES)), [last])], found)
+    found = maxima([([QUERIES - 2], first)], found)
+    found = maxima([(list(range(QUERIES - 1)), [last])], found)
+    found = maxima([([QUERIES - 1], first + [last])], found)
     home = lax.all_to_all(
         found, ("grp", "mem"), split_axis=0, concat_axis=0, tiled=True
     )

time: 41 us -> 39 us (0.951)
  starting transfers between devices: 16.1 us -> 13.8 us
  waiting for transfers between devices: 7.41 us -> 8.87 us
  Pallas kernels: 2.27 us -> 3.71 us
  blocking collectives: 12.7 us -> 11.7 us
  local copies, waits for them, and re-layouts: 0.95 us -> 0 us
  other arithmetic: 1.23 us -> 0.56 us
    ppermute x9, starting transfers between devices: 16.1 us -> 13.8 us  [send(): return lax.ppermute(value, ('grp', 'mem'), route)]
    ppermute x9, waiting for transfers between devices: 7.41 us -> 8.87 us  [send(): return lax.ppermute(value, ('grp', 'mem'), route)]
    pallas_call x1, Pallas kernels: 0.14 us -> 1.32 us  [body(): pl.pallas_call(prepare_kernel, out_shape=jax.ShapeDtypeStruct((width + ME...]
    unnamed x2 -> x0, local copies, waits for them, and re-layouts: 0.95 us -> none
    all_to_all x1, blocking collectives: 12.7 us -> 11.7 us  [body(): lax.all_to_all(found, ('grp', 'mem'), split_axis=0, concat_axis=0, tiled=...]
    reshape x1 -> x0, other arithmetic: 0.68 us -> none  [body(): key.reshape(1, rows)]
    pallas_call x3 -> x4, Pallas kernels: 2.13 us -> 2.39 us  [maxima(): pl.pallas_call(functools.partial(similarity_kernel, work, used_queries, u...]
  transfers between devices with their start and end apart: 9 -> 9, of which waited for: 2 -> 3; matrix products, arithmetic and copies ran while one was open for 0% -> 0% of each run, Pallas kernels for 3% -> 5%
where the time goes in v2:
time: 39 us; the launch traced here: 38.8 us
  starting transfers between devices  13.8 us (35%)
  blocking collectives  11.7 us (30%)
  waiting for transfers between devices  8.87 us (23%)
  Pallas kernels  3.71 us (10%)
  other arithmetic  0.56 us (1%)
    ppermute x9, starting transfers between devices, send(): return lax.ppermute(value, ('grp', 'mem'), route)  13.8 us
    all_to_all x1, blocking collectives, body(): lax.all_to_all(found, ('grp', 'mem'), split_axis=0, concat_axis=0, tiled=...  11.7 us
    ppermute x9, waiting for transfers between devices, send(): return lax.ppermute(value, ('grp', 'mem'), route)  8.87 us
    pallas_call x4, Pallas kernels, maxima(): pl.pallas_call(functools.partial(similarity_kernel, work, used_queries, u...  2.39 us
    pallas_call x1, Pallas kernels, body(): pl.pallas_call(prepare_kernel, out_shape=jax.ShapeDtypeStruct((width + ME...  1.32 us
  transfers between devices with their start and end apart: 9, of which 3 were waited for; matrix products, arithmetic and copies ran while one was open for 0% of the time, Pallas kernels for 5%

profile of v2, /device:TPU:0, one launch (start us, length us, event | category | flops | bytes accessed | tf_op | source)
XLA Modules:
  0.0 38.8 jit_solution(6773278335300651773)
XLA Ops:
  0.0 1.3 %prepare.1.refs_0_.refs_6_.refs_1_ = bf16[1040,128]{1,0:T(8,128)(2,1)S(1)} custom-call(bf16[128,1024]{1,0:T(8,128)(2,1)} %x_ref.1, s32[1,128]{1,0:T(1,128)} %bitcast.6, s32[1,128]{1,0:T(1,128)} %bitcast.7), custom_call_target="tpu_custom_call" | custom-call | tf_op jit(solution)/shard_map/prepare/pallas_call | solution.py:165
  1.3 0.6 %collective-permute-start.4 = (bf16[1040,128]{1,0:T(8,128)(2,1)S(1)}, bf16[1040,128]{1,0:T(8,128)(2,1)S(1)}, u32[]{:S(2)}, u32[]{:S(2)}) collective-permute-start(bf16[1040,128]{1,0:T(8,128)(2,1)S(1)} %prepare.1.refs_0_.refs_6_.refs_1_), channel_id=1, source_target_pairs={{0,1},{1,0},{2,3},{3,2},{4,5},{5,4},{6,7},{7,6},{8,9},{9,8},{10,11... | collective-permute-start | bytes 798728 | tf_op jit(solution)/shard_map/ppermute | solution.py:183
  1.9 2.6 %collective-permute-start = (bf16[1040,128]{1,0:T(8,128)(2,1)S(1)}, bf16[1040,128]{1,0:T(8,128)(2,1)S(1)}, u32[]{:S(2)}, u32[]{:S(2)}) collective-permute-start(bf16[1040,128]{1,0:T(8,128)(2,1)S(1)} %prepare.1.refs_0_.refs_6_.refs_1_), channel_id=1, source_target_pairs={{0,8},{1,17},{2,10},{3,19},{4,12},{5,21},{6,14},{7,23},{8,0},{9,25... | collective-permute-start | bytes 798728 | tf_op jit(solution)/shard_map/ppermute | solution.py:183
  4.4 0.0 collective-permute-done.4.refs_1_
  4.4 1.5 %collective-permute-start.6 = (bf16[1040,128]{1,0:T(8,128)(2,1)S(1)}, bf16[1040,128]{1,0:T(8,128)(2,1)S(1)}, u32[]{:S(2)}, u32[]{:S(2)}) collective-permute-start(bf16[1040,128]{1,0:T(8,128)(2,1)S(1)} %collective-permute-done.4.refs_1_), channel_id=1, source_target_pairs={{0,8},{1,17},{2,10},{3,19},{4,12},{5,21},{6,14},{7,23},{8,0},{9,25... | collective-permute-start | bytes 798728 | tf_op jit(solution)/shard_map/ppermute | solution.py:183
  5.9 2.9 %collective-permute-done.refs_2_ = bf16[1040,128]{1,0:T(8,128)(2,1)S(1)} collective-permute-done((bf16[1040,128]{1,0:T(8,128)(2,1)S(1)}, bf16[1040,128]{1,0:T(8,128)(2,1)S(1)}, u32[]{:S(2)}, u32[]{:S(2)}) %collective-permute-start) | collective-permute-done | bytes 266272 | tf_op jit(solution)/shard_map/ppermute | solution.py:183
  8.8 2.0 %collective-permute-start.1 = (bf16[1040,128]{1,0:T(8,128)(2,1)S(1)}, bf16[1040,128]{1,0:T(8,128)(2,1)S(1)}, u32[]{:S(2)}, u32[]{:S(2)}) collective-permute-start(bf16[1040,128]{1,0:T(8,128)(2,1)S(1)} %collective-permute-done.refs_2_), channel_id=1, source_target_pairs={{0,16},{1,9},{2,18},{3,11},{4,20},{5,13},{6,22},{7,15},{8,24},{9,1... | collective-permute-start | bytes 798728 | tf_op jit(solution)/shard_map/ppermute | solution.py:183
  10.9 4.5 %collective-permute-start.3 = (bf16[1040,128]{1,0:T(8,128)(2,1)S(1)}, bf16[1040,128]{1,0:T(8,128)(2,1)S(1)}, u32[]{:S(2)}, u32[]{:S(2)}) collective-permute-start(bf16[1040,128]{1,0:T(8,128)(2,1)S(1)} %prepare.1.refs_0_.refs_6_.refs_1_), channel_id=1, source_target_pairs={{0,4},{6,2},{1,3},{3,5},{5,7},{7,1},{8,12},{14,10},{9,11},{11,13},... | collective-permute-start | bytes 798728 | tf_op jit(solution)/shard_map/ppermute | solution.py:183
  15.4 0.1 collective-permute-start.7
  15.5 0.0 collective-permute-done.6.refs_3_
  15.5 0.5 %collective-permute-start.8 = (bf16[1040,128]{1,0:T(8,128)(2,1)S(1)}, bf16[1040,128]{1,0:T(8,128)(2,1)S(1)}, u32[]{:S(2)}, u32[]{:S(2)}) collective-permute-start(bf16[1040,128]{1,0:T(8,128)(2,1)S(1)} %collective-permute-done.6.refs_3_), channel_id=1, source_target_pairs={{0,1},{1,0},{2,3},{3,2},{4,5},{5,4},{6,7},{7,6},{8,9},{9,8},{10,11... | collective-permute-start | bytes 798728 | tf_op jit(solution)/shard_map/ppermute | solution.py:183
  16.0 2.0 %collective-permute-start.5 = (bf16[1040,128]{1,0:T(8,128)(2,1)S(1)}, bf16[1040,128]{1,0:T(8,128)(2,1)S(1)}, u32[]{:S(2)}, u32[]{:S(2)}) collective-permute-start(bf16[1040,128]{1,0:T(8,128)(2,1)S(1)} %collective-permute-done.4.refs_1_), channel_id=1, source_target_pairs={{0,4},{6,2},{1,3},{3,5},{5,7},{7,1},{8,12},{14,10},{9,11},{11,13},... | collective-permute-start | bytes 798728 | tf_op jit(solution)/shard_map/ppermute | solution.py:183
  18.0 0.0 collective-permute-done.1.refs_0_.refs_6_
  18.0 0.1 collective-permute-start.2
  18.1 2.5 %collective-permute-done.3.refs_7_.refs_2_ = bf16[1040,128]{1,0:T(8,128)(2,1)S(1)} collective-permute-done((bf16[1040,128]{1,0:T(8,128)(2,1)S(1)}, bf16[1040,128]{1,0:T(8,128)(2,1)S(1)}, u32[]{:S(2)}, u32[]{:S(2)}) %collective-permute-start.3) | collective-permute-done | bytes 266272 | tf_op jit(solution)/shard_map/ppermute | solution.py:183
  20.6 0.0 collective-permute-done.7.refs_4_
  20.6 0.0 collective-permute-done.8.refs_5_
  20.6 0.8 %shard_map.37.refs_3_ = f32[32,128]{1,0:T(8,128)S(1)} custom-call(bf16[1040,128]{1,0:T(8,128)(2,1)S(1)} %prepare.1.refs_0_.refs_6_.refs_1_, bf16[1040,128]{1,0:T(8,128)(2,1)S(1)} %collective-permute-done.4.refs_1_, bf16[1040,128]{1,0:T(8,128)(2,1)S(1)} %collective-permute-done.refs_2_, bf16[1040,128]{1,0:T(8,128)(2,1)S(1)} %collective-permute-done.6.refs_3_, ...), custom_call_target="tpu_custom_call" | custom-call | flops 402653184 | tf_op jit(solution)/shard_map/pallas_call | solution.py:231
  21.4 0.4 shard_map.38.refs_8_
  21.8 3.4 %collective-permute-done.5.refs_7_.refs_3_ = bf16[1040,128]{1,0:T(8,128)(2,1)S(1)} collective-permute-done((bf16[1040,128]{1,0:T(8,128)(2,1)S(1)}, bf16[1040,128]{1,0:T(8,128)(2,1)S(1)}, u32[]{:S(2)}, u32[]{:S(2)}) %collective-permute-start.5) | collective-permute-done | bytes 266272 | tf_op jit(solution)/shard_map/ppermute | solution.py:183
  25.2 0.8 %shard_map.39.refs_4_ = f32[32,128]{1,0:T(8,128)S(1)} custom-call(bf16[1040,128]{1,0:T(8,128)(2,1)S(1)} %prepare.1.refs_0_.refs_6_.refs_1_, bf16[1040,128]{1,0:T(8,128)(2,1)S(1)} %collective-permute-done.4.refs_1_, bf16[1040,128]{1,0:T(8,128)(2,1)S(1)} %collective-permute-done.refs_2_, bf16[1040,128]{1,0:T(8,128)(2,1)S(1)} %collective-permute-done.6.refs_3_, ...), custom_call_target="tpu_custom_call" | custom-call | flops 234881024 | tf_op jit(solution)/shard_map/pallas_call | solution.py:231
  26.0 0.0 collective-permute-done.2.refs_0_
  26.0 0.4 %shard_map.40 = f32[32,128]{1,0:T(8,128)S(1)} custom-call(bf16[1040,128]{1,0:T(8,128)(2,1)S(1)} %collective-permute-done.2.refs_0_, bf16[1040,128]{1,0:T(8,128)(2,1)S(1)} %prepare.1.refs_0_.refs_6_.refs_1_, bf16[1040,128]{1,0:T(8,128)(2,1)S(1)} %collective-permute-done.3.refs_7_.refs_2_, bf16[1040,128]{1,0:T(8,128)(2,1)S(1)} %collective-permute-done.5.refs_7_.refs_3_, ...), custom_call_target="tpu_custom_call" | custom-call | flops 100663296 | tf_op jit(solution)/shard_map/pallas_call | solution.py:231
  26.5 11.7 %all_to_all.9 = f32[32,1,128]{2,1,0:T(1,128)S(1)} all-to-all(f32[32,1,128]{2,1,0:T(1,128)S(1)} %bitcast.5), channel_id=1, replica_groups=mesh['grp'=4,'mem'=8] {'grp','mem'}, dimensions={0} | all-to-all | bytes 32768 | tf_op jit(solution)/shard_map/all_to_all | solution.py:259
  38.2 0.6 %reduce_max.9 = f32[128]{0:T(128)} reduce(f32[32,1,128]{2,1,0:T(1,128)S(1)} %all_to_all.9, f32[]{:T(128)} %constant.0.clone.1), dimensions={0,1}, to_apply=%region_0.0 | reduce | flops 3968 | bytes 16900 | tf_op jit(solution)/shard_map/reduce_max | solution.py:262
Async XLA Ops:
  1.3 3.1 %collective-permute-start.4 = (bf16[1040,128]{1,0:T(8,128)(2,1)S(1)}, bf16[1040,128]{1,0:T(8,128)(2,1)S(1)}, u32[]{:S(2)}, u32[]{:S(2)}) collective-permute-start(bf16[1040,128]{1,0:T(8,128)(2,1)S(1)} %prepare.1.refs_0_.refs_6_.refs_1_), channel_id=1, source_target_pairs={{0,1},{1,0},{2,3},{3,2},{4,5},{5,4},{6,7},{7,6},{8,9},{9,8},{10,11... | collective-permute-start | bytes 798728 | tf_op jit(solution)/shard_map/ppermute | solution.py:183
  1.9 6.9 %collective-permute-start = (bf16[1040,128]{1,0:T(8,128)(2,1)S(1)}, bf16[1040,128]{1,0:T(8,128)(2,1)S(1)}, u32[]{:S(2)}, u32[]{:S(2)}) collective-permute-start(bf16[1040,128]{1,0:T(8,128)(2,1)S(1)} %prepare.1.refs_0_.refs_6_.refs_1_), channel_id=1, source_target_pairs={{0,8},{1,17},{2,10},{3,19},{4,12},{5,21},{6,14},{7,23},{8,0},{9,25... | collective-permute-start | bytes 798728 | tf_op jit(solution)/shard_map/ppermute | solution.py:183
  4.4 11.0 %collective-permute-start.6 = (bf16[1040,128]{1,0:T(8,128)(2,1)S(1)}, bf16[1040,128]{1,0:T(8,128)(2,1)S(1)}, u32[]{:S(2)}, u32[]{:S(2)}) collective-permute-start(bf16[1040,128]{1,0:T(8,128)(2,1)S(1)} %collective-permute-done.4.refs_1_), channel_id=1, source_target_pairs={{0,8},{1,17},{2,10},{3,19},{4,12},{5,21},{6,14},{7,23},{8,0},{9,25... | collective-permute-start | bytes 798728 | tf_op jit(solution)/shard_map/ppermute | solution.py:183
  8.8 9.2 %collective-permute-start.1 = (bf16[1040,128]{1,0:T(8,128)(2,1)S(1)}, bf16[1040,128]{1,0:T(8,128)(2,1)S(1)}, u32[]{:S(2)}, u32[]{:S(2)}) collective-permute-start(bf16[1040,128]{1,0:T(8,128)(2,1)S(1)} %collective-permute-done.refs_2_), channel_id=1, source_target_pairs={{0,16},{1,9},{2,18},{3,11},{4,20},{5,13},{6,22},{7,15},{8,24},{9,1... | collective-permute-start | bytes 798728 | tf_op jit(solution)/shard_map/ppermute | solution.py:183
  10.9 9.7 %collective-permute-start.3 = (bf16[1040,128]{1,0:T(8,128)(2,1)S(1)}, bf16[1040,128]{1,0:T(8,128)(2,1)S(1)}, u32[]{:S(2)}, u32[]{:S(2)}) collective-permute-start(bf16[1040,128]{1,0:T(8,128)(2,1)S(1)} %prepare.1.refs_0_.refs_6_.refs_1_), channel_id=1, source_target_pairs={{0,4},{6,2},{1,3},{3,5},{5,7},{7,1},{8,12},{14,10},{9,11},{11,13},... | collective-permute-start | bytes 798728 | tf_op jit(solution)/shard_map/ppermute | solution.py:183
  15.4 5.2 %collective-permute-start.7 = (bf16[1040,128]{1,0:T(8,128)(2,1)S(1)}, bf16[1040,128]{1,0:T(8,128)(2,1)S(1)}, u32[]{:S(2)}, u32[]{:S(2)}) collective-permute-start(bf16[1040,128]{1,0:T(8,128)(2,1)S(1)} %collective-permute-done.refs_2_), channel_id=1, source_target_pairs={{0,1},{1,0},{2,3},{3,2},{4,5},{5,4},{6,7},{7,6},{8,9},{9,8},{10,11... | collective-permute-start | bytes 798728 | tf_op jit(solution)/shard_map/ppermute | solution.py:183
  15.5 5.1 %collective-permute-start.8 = (bf16[1040,128]{1,0:T(8,128)(2,1)S(1)}, bf16[1040,128]{1,0:T(8,128)(2,1)S(1)}, u32[]{:S(2)}, u32[]{:S(2)}) collective-permute-start(bf16[1040,128]{1,0:T(8,128)(2,1)S(1)} %collective-permute-done.6.refs_3_), channel_id=1, source_target_pairs={{0,1},{1,0},{2,3},{3,2},{4,5},{5,4},{6,7},{7,6},{8,9},{9,8},{10,11... | collective-permute-start | bytes 798728 | tf_op jit(solution)/shard_map/ppermute | solution.py:183
  16.0 9.2 %collective-permute-start.5 = (bf16[1040,128]{1,0:T(8,128)(2,1)S(1)}, bf16[1040,128]{1,0:T(8,128)(2,1)S(1)}, u32[]{:S(2)}, u32[]{:S(2)}) collective-permute-start(bf16[1040,128]{1,0:T(8,128)(2,1)S(1)} %collective-permute-done.4.refs_1_), channel_id=1, source_target_pairs={{0,4},{6,2},{1,3},{3,5},{5,7},{7,1},{8,12},{14,10},{9,11},{11,13},... | collective-permute-start | bytes 798728 | tf_op jit(solution)/shard_map/ppermute | solution.py:183
  18.0 8.0 %collective-permute-start.2 = (bf16[1040,128]{1,0:T(8,128)(2,1)S(1)}, bf16[1040,128]{1,0:T(8,128)(2,1)S(1)}, u32[]{:S(2)}, u32[]{:S(2)}) collective-permute-start(bf16[1040,128]{1,0:T(8,128)(2,1)S(1)} %collective-permute-done.1.refs_0_.refs_6_), channel_id=1, source_target_pairs={{0,1},{1,0},{2,3},{3,2},{4,5},{5,4},{6,7},{7,6},{8,9},{9,8},{10,11... | collective-permute-start | bytes 798728 | tf_op jit(solution)/shard_map/ppermute | solution.py:183

commit v3 on v2

--- a/solution.py
+++ b/solution.py
@@ -10,7 +10,6 @@
 
 META = 16
 QUERIES = 8
-CHUNKS = 4
 SHIFT = 21
 
 
@@ -25,32 +24,21 @@
 
 
 def prepare_kernel(x_ref, cluster_ref, rank_ref, out_ref, x_buf, meta_buf, sems):
-    rows = x_ref.shape[0]
-    part = rows // CHUNKS
+    rows, width = x_ref.shape
     loads = [
-        pltpu.make_async_copy(
-            x_ref.at[pl.ds(i * part, part), :],
-            x_buf.at[pl.ds(i * part, part), :],
-            sems.at[i],
-        )
-        for i in range(CHUNKS)
-    ]
-    loads.append(pltpu.make_async_copy(cluster_ref, meta_buf.at[0], sems.at[CHUNKS]))
-    loads.append(pltpu.make_async_copy(rank_ref, meta_buf.at[1], sems.at[CHUNKS + 1]))
+        pltpu.make_async_copy(x_ref, x_buf, sems.at[0]),
+        pltpu.make_async_copy(cluster_ref, meta_buf.at[0], sems.at[1]),
+        pltpu.make_async_copy(rank_ref, meta_buf.at[1], sems.at[2]),
+    ]
     for load in loads:
         load.start()
-    width = x_ref.shape[1]
-    for i in range(CHUNKS):
-        loads[i].wait()
-        wide = x_buf[i * part : (i + 1) * part, :].astype(jnp.float32)
-        scale = lax.rsqrt(jnp.sum(wide * wide, axis=1, keepdims=True) + 1e-06)
-        narrow = (wide * scale).astype(jnp.bfloat16)
-        for start in range(0, width, rows):
-            out_ref[start + i * part : start + (i + 1) * part, :] = narrow[
-                :, start : start + rows
-            ]
-    loads[CHUNKS].wait()
-    loads[CHUNKS + 1].wait()
+    for load in loads:
+        load.wait()
+    wide = x_buf[...].astype(jnp.float32)
+    scale = lax.rsqrt(jnp.sum(wide * wide, axis=1, keepdims=True) + 1e-06)
+    normed = (wide * scale).astype(jnp.bfloat16)
+    for start in range(0, width, rows):
+        out_ref[start : start + rows, :] = normed[:, start : start + rows]
     key = meta_buf[0] * (1 << SHIFT) + meta_buf[1] + 1
     digit = lax.broadcasted_iota(jnp.int32, (META, rows), 0)
     spread = jnp.where(
@@ -118,34 +106,52 @@
     query_places, key_places = places_of(members, pairs)
     slot_of = lax.broadcasted_iota(jnp.int32, out_ref.shape, 0)
     result = refs[-2][...] if has_before else jnp.full(out_ref.shape, -1.0, jnp.float32)
+    upright = len(queries) < len(keys)
     query_keys = {j: keys_of(q) for j, q in queries.items()}
-    other_keys = {i: [column(v) for v in keys_of(k)] for i, k in keys.items()}
+    other_keys = {i: keys_of(k) for i, k in keys.items()}
+    tall = query_keys if upright else other_keys
+    for name, pair in tall.items():
+        tall[name] = [column(value) for value in pair]
     best = {}
     back = {}
+
+    def gather(found, name, mask, tile):
+        tile = jnp.where(mask, tile, -1.0)
+        found[name] = jnp.maximum(found[name], tile) if name in found else tile
+
+    def panel(blocks, names):
+        return jnp.concatenate([rows_of(blocks[name]) for name in names], axis=0)
+
     for query_list, key_list in groups:
-        other_rows = jnp.concatenate([rows_of(keys[i]) for i in key_list], axis=0)
-        for start in range(0, len(query_list), 2):
-            some = query_list[start : start + 2]
-            query_rows = jnp.concatenate([rows_of(queries[j]) for j in some], axis=0)
+        down, along = (queries, keys) if upright else (keys, queries)
+        down_list, along_list = (
+            (query_list, key_list) if upright else (key_list, query_list)
+        )
+        down_rows = panel(down, down_list)
+        for start in range(0, len(along_list), 2):
+            some = along_list[start : start + 2]
             gram = lax.dot_general(
-                other_rows,
-                query_rows,
+                down_rows,
+                panel(along, some),
                 (((1,), (1,)), ((), ())),
                 preferred_element_type=jnp.float32,
             )
-            for a, i in enumerate(key_list):
-                key, owner = other_keys[i]
-                for b, j in enumerate(some):
+            for a, d in enumerate(down_list):
+                for b, w in enumerate(some):
+                    j, i = (d, w) if upright else (w, d)
                     query_key, query_owner = query_keys[j]
+                    key, owner = other_keys[i]
                     tile = gram[a * rows : (a + 1) * rows, b * rows : (b + 1) * rows]
                     same = owner == query_owner
-                    found = jnp.where(same & (key < query_key), tile, -1.0)
-                    best[j] = jnp.maximum(best[j], found) if j in best else found
+                    gather(best, j, same & (key < query_key), tile)
                     if key_places[i] is not None:
-                        found = jnp.where(same & (query_key < key), tile, -1.0)
-                        back[i] = jnp.maximum(back[i], found) if i in back else found
-    maxima = [(query_places[j], value) for j, value in best.items()]
-    maxima += [(key_places[i], value.T) for i, value in back.items()]
+                        gather(back, i, same & (query_key < key), tile)
+    maxima = [
+        (query_places[j], value.T if upright else value) for j, value in best.items()
+    ]
+    maxima += [
+        (key_places[i], value if upright else value.T) for i, value in back.items()
+    ]
     for place, value in maxima:
         result = jnp.maximum(
             result,
@@ -170,7 +176,7 @@
         scratch_shapes=[
             pltpu.VMEM((rows, width), jnp.bfloat16),
             pltpu.VMEM((2, 1, rows), jnp.int32),
-            pltpu.SemaphoreType.DMA((CHUNKS + 2,)),
+            pltpu.SemaphoreType.DMA((3,)),
         ],
         compiler_params=pltpu.CompilerParams(vmem_limit_bytes=4 << 20),
         name="prepare",

time: 39 us -> 38.8 us (level)
  no operation moved by 1% of the time
where the time goes in v3:
time: 38.8 us; the launch traced here: 38.6 us
  starting transfers between devices  13.8 us (36%)
  blocking collectives  11.7 us (30%)
  waiting for transfers between devices  8.87 us (23%)
  Pallas kernels  3.53 us (9%)
  other arithmetic  0.56 us (1%)
    ppermute x9, starting transfers between devices, send(): return lax.ppermute(value, ('grp', 'mem'), route)  13.8 us
    all_to_all x1, blocking collectives, body(): lax.all_to_all(found, ('grp', 'mem'), split_axis=0, concat_axis=0, tiled=...  11.7 us
    ppermute x9, waiting for transfers between devices, send(): return lax.ppermute(value, ('grp', 'mem'), route)  8.87 us
    pallas_call x4, Pallas kernels, maxima(): pl.pallas_call(functools.partial(similarity_kernel, work, used_queries, u...  2.41 us
    pallas_call x1, Pallas kernels, body(): pl.pallas_call(prepare_kernel, out_shape=jax.ShapeDtypeStruct((width + ME...  1.12 us
  transfers between devices with their start and end apart: 9, of which 3 were waited for; matrix products, arithmetic and copies ran while one was open for 0% of the time, Pallas kernels for 5%

profile of v3, /device:TPU:0, one launch (start us, length us, event | category | flops | bytes accessed | tf_op | source)
XLA Modules:
  0.0 38.6 jit_solution(14723396698798817491)
XLA Ops:
  0.0 1.1 %prepare.1.refs_0_.refs_6_.refs_1_ = bf16[1040,128]{1,0:T(8,128)(2,1)S(1)} custom-call(bf16[128,1024]{1,0:T(8,128)(2,1)} %x_ref.1, s32[1,128]{1,0:T(1,128)} %bitcast.6, s32[1,128]{1,0:T(1,128)} %bitcast.7), custom_call_target="tpu_custom_call" | custom-call | tf_op jit(solution)/shard_map/prepare/pallas_call | solution.py:171
  1.1 0.6 %collective-permute-start.4 = (bf16[1040,128]{1,0:T(8,128)(2,1)S(1)}, bf16[1040,128]{1,0:T(8,128)(2,1)S(1)}, u32[]{:S(2)}, u32[]{:S(2)}) collective-permute-start(bf16[1040,128]{1,0:T(8,128)(2,1)S(1)} %prepare.1.refs_0_.refs_6_.refs_1_), channel_id=1, source_target_pairs={{0,1},{1,0},{2,3},{3,2},{4,5},{5,4},{6,7},{7,6},{8,9},{9,8},{10,11... | collective-permute-start | bytes 798728 | tf_op jit(solution)/shard_map/ppermute | solution.py:189
  1.7 2.6 %collective-permute-start = (bf16[1040,128]{1,0:T(8,128)(2,1)S(1)}, bf16[1040,128]{1,0:T(8,128)(2,1)S(1)}, u32[]{:S(2)}, u32[]{:S(2)}) collective-permute-start(bf16[1040,128]{1,0:T(8,128)(2,1)S(1)} %prepare.1.refs_0_.refs_6_.refs_1_), channel_id=1, source_target_pairs={{0,8},{1,17},{2,10},{3,19},{4,12},{5,21},{6,14},{7,23},{8,0},{9,25... | collective-permute-start | bytes 798728 | tf_op jit(solution)/shard_map/ppermute | solution.py:189
  4.2 0.0 collective-permute-done.4.refs_1_
  4.2 1.5 %collective-permute-start.6 = (bf16[1040,128]{1,0:T(8,128)(2,1)S(1)}, bf16[1040,128]{1,0:T(8,128)(2,1)S(1)}, u32[]{:S(2)}, u32[]{:S(2)}) collective-permute-start(bf16[1040,128]{1,0:T(8,128)(2,1)S(1)} %collective-permute-done.4.refs_1_), channel_id=1, source_target_pairs={{0,8},{1,17},{2,10},{3,19},{4,12},{5,21},{6,14},{7,23},{8,0},{9,25... | collective-permute-start | bytes 798728 | tf_op jit(solution)/shard_map/ppermute | solution.py:189
  5.7 2.9 %collective-permute-done.refs_2_ = bf16[1040,128]{1,0:T(8,128)(2,1)S(1)} collective-permute-done((bf16[1040,128]{1,0:T(8,128)(2,1)S(1)}, bf16[1040,128]{1,0:T(8,128)(2,1)S(1)}, u32[]{:S(2)}, u32[]{:S(2)}) %collective-permute-start) | collective-permute-done | bytes 266272 | tf_op jit(solution)/shard_map/ppermute | solution.py:189
  8.6 2.0 %collective-permute-start.1 = (bf16[1040,128]{1,0:T(8,128)(2,1)S(1)}, bf16[1040,128]{1,0:T(8,128)(2,1)S(1)}, u32[]{:S(2)}, u32[]{:S(2)}) collective-permute-start(bf16[1040,128]{1,0:T(8,128)(2,1)S(1)} %collective-permute-done.refs_2_), channel_id=1, source_target_pairs={{0,16},{1,9},{2,18},{3,11},{4,20},{5,13},{6,22},{7,15},{8,24},{9,1... | collective-permute-start | bytes 798728 | tf_op jit(solution)/shard_map/ppermute | solution.py:189
  10.7 4.5 %collective-permute-start.3 = (bf16[1040,128]{1,0:T(8,128)(2,1)S(1)}, bf16[1040,128]{1,0:T(8,128)(2,1)S(1)}, u32[]{:S(2)}, u32[]{:S(2)}) collective-permute-start(bf16[1040,128]{1,0:T(8,128)(2,1)S(1)} %prepare.1.refs_0_.refs_6_.refs_1_), channel_id=1, source_target_pairs={{0,4},{6,2},{1,3},{3,5},{5,7},{7,1},{8,12},{14,10},{9,11},{11,13},... | collective-permute-start | bytes 798728 | tf_op jit(solution)/shard_map/ppermute | solution.py:189
  15.2 0.1 collective-permute-start.7
  15.3 0.0 collective-permute-done.6.refs_3_
  15.3 0.5 %collective-permute-start.8 = (bf16[1040,128]{1,0:T(8,128)(2,1)S(1)}, bf16[1040,128]{1,0:T(8,128)(2,1)S(1)}, u32[]{:S(2)}, u32[]{:S(2)}) collective-permute-start(bf16[1040,128]{1,0:T(8,128)(2,1)S(1)} %collective-permute-done.6.refs_3_), channel_id=1, source_target_pairs={{0,1},{1,0},{2,3},{3,2},{4,5},{5,4},{6,7},{7,6},{8,9},{9,8},{10,11... | collective-permute-start | bytes 798728 | tf_op jit(solution)/shard_map/ppermute | solution.py:189
  15.8 2.0 %collective-permute-start.5 = (bf16[1040,128]{1,0:T(8,128)(2,1)S(1)}, bf16[1040,128]{1,0:T(8,128)(2,1)S(1)}, u32[]{:S(2)}, u32[]{:S(2)}) collective-permute-start(bf16[1040,128]{1,0:T(8,128)(2,1)S(1)} %collective-permute-done.4.refs_1_), channel_id=1, source_target_pairs={{0,4},{6,2},{1,3},{3,5},{5,7},{7,1},{8,12},{14,10},{9,11},{11,13},... | collective-permute-start | bytes 798728 | tf_op jit(solution)/shard_map/ppermute | solution.py:189
  17.8 0.0 collective-permute-done.1.refs_0_.refs_6_
  17.8 0.1 collective-permute-start.2
  17.9 2.5 %collective-permute-done.3.refs_7_.refs_2_ = bf16[1040,128]{1,0:T(8,128)(2,1)S(1)} collective-permute-done((bf16[1040,128]{1,0:T(8,128)(2,1)S(1)}, bf16[1040,128]{1,0:T(8,128)(2,1)S(1)}, u32[]{:S(2)}, u32[]{:S(2)}) %collective-permute-start.3) | collective-permute-done | bytes 266272 | tf_op jit(solution)/shard_map/ppermute | solution.py:189
  20.4 0.0 collective-permute-done.7.refs_4_
  20.4 0.0 collective-permute-done.8.refs_5_
  20.4 0.8 %shard_map.37.refs_3_ = f32[32,128]{1,0:T(8,128)S(1)} custom-call(bf16[1040,128]{1,0:T(8,128)(2,1)S(1)} %prepare.1.refs_0_.refs_6_.refs_1_, bf16[1040,128]{1,0:T(8,128)(2,1)S(1)} %collective-permute-done.4.refs_1_, bf16[1040,128]{1,0:T(8,128)(2,1)S(1)} %collective-permute-done.refs_2_, bf16[1040,128]{1,0:T(8,128)(2,1)S(1)} %collective-permute-done.6.refs_3_, ...), custom_call_target="tpu_custom_call" | custom-call | flops 402653184 | tf_op jit(solution)/shard_map/pallas_call | solution.py:237
  21.2 0.4 %shard_map.38.refs_8_ = f32[32,128]{1,0:T(8,128)S(1)} custom-call(bf16[1040,128]{1,0:T(8,128)(2,1)S(1)} %collective-permute-done.1.refs_0_.refs_6_, bf16[1040,128]{1,0:T(8,128)(2,1)S(1)} %prepare.1.refs_0_.refs_6_.refs_1_, bf16[1040,128]{1,0:T(8,128)(2,1)S(1)} %collective-permute-done.3.refs_7_.refs_2_, f32[32,128]{1,0:T(8,128)S(1)} %shard_map.37.refs_3_), custom_call_target="tpu_custom_call" | custom-call | flops 67108864 | tf_op jit(solution)/shard_map/pallas_call | solution.py:237
  21.6 3.4 %collective-permute-done.5.refs_7_.refs_3_ = bf16[1040,128]{1,0:T(8,128)(2,1)S(1)} collective-permute-done((bf16[1040,128]{1,0:T(8,128)(2,1)S(1)}, bf16[1040,128]{1,0:T(8,128)(2,1)S(1)}, u32[]{:S(2)}, u32[]{:S(2)}) %collective-permute-start.5) | collective-permute-done | bytes 266272 | tf_op jit(solution)/shard_map/ppermute | solution.py:189
  25.0 0.8 %shard_map.39.refs_4_ = f32[32,128]{1,0:T(8,128)S(1)} custom-call(bf16[1040,128]{1,0:T(8,128)(2,1)S(1)} %prepare.1.refs_0_.refs_6_.refs_1_, bf16[1040,128]{1,0:T(8,128)(2,1)S(1)} %collective-permute-done.4.refs_1_, bf16[1040,128]{1,0:T(8,128)(2,1)S(1)} %collective-permute-done.refs_2_, bf16[1040,128]{1,0:T(8,128)(2,1)S(1)} %collective-permute-done.6.refs_3_, ...), custom_call_target="tpu_custom_call" | custom-call | flops 234881024 | tf_op jit(solution)/shard_map/pallas_call | solution.py:237
  25.8 0.0 collective-permute-done.2.refs_0_
  25.8 0.5 %shard_map.40 = f32[32,128]{1,0:T(8,128)S(1)} custom-call(bf16[1040,128]{1,0:T(8,128)(2,1)S(1)} %collective-permute-done.2.refs_0_, bf16[1040,128]{1,0:T(8,128)(2,1)S(1)} %prepare.1.refs_0_.refs_6_.refs_1_, bf16[1040,128]{1,0:T(8,128)(2,1)S(1)} %collective-permute-done.3.refs_7_.refs_2_, bf16[1040,128]{1,0:T(8,128)(2,1)S(1)} %collective-permute-done.5.refs_7_.refs_3_, ...), custom_call_target="tpu_custom_call" | custom-call | flops 100663296 | tf_op jit(solution)/shard_map/pallas_call | solution.py:237
  26.3 11.7 %all_to_all.9 = f32[32,1,128]{2,1,0:T(1,128)S(1)} all-to-all(f32[32,1,128]{2,1,0:T(1,128)S(1)} %bitcast.5), channel_id=1, replica_groups=mesh['grp'=4,'mem'=8] {'grp','mem'}, dimensions={0} | all-to-all | bytes 32768 | tf_op jit(solution)/shard_map/all_to_all | solution.py:265
  38.0 0.6 %reduce_max.9 = f32[128]{0:T(128)} reduce(f32[32,1,128]{2,1,0:T(1,128)S(1)} %all_to_all.9, f32[]{:T(128)} %constant.0.clone.1), dimensions={0,1}, to_apply=%region_0.0 | reduce | flops 3968 | bytes 16900 | tf_op jit(solution)/shard_map/reduce_max | solution.py:268
Async XLA Ops:
  1.1 3.1 %collective-permute-start.4 = (bf16[1040,128]{1,0:T(8,128)(2,1)S(1)}, bf16[1040,128]{1,0:T(8,128)(2,1)S(1)}, u32[]{:S(2)}, u32[]{:S(2)}) collective-permute-start(bf16[1040,128]{1,0:T(8,128)(2,1)S(1)} %prepare.1.refs_0_.refs_6_.refs_1_), channel_id=1, source_target_pairs={{0,1},{1,0},{2,3},{3,2},{4,5},{5,4},{6,7},{7,6},{8,9},{9,8},{10,11... | collective-permute-start | bytes 798728 | tf_op jit(solution)/shard_map/ppermute | solution.py:189
  1.7 6.9 %collective-permute-start = (bf16[1040,128]{1,0:T(8,128)(2,1)S(1)}, bf16[1040,128]{1,0:T(8,128)(2,1)S(1)}, u32[]{:S(2)}, u32[]{:S(2)}) collective-permute-start(bf16[1040,128]{1,0:T(8,128)(2,1)S(1)} %prepare.1.refs_0_.refs_6_.refs_1_), channel_id=1, source_target_pairs={{0,8},{1,17},{2,10},{3,19},{4,12},{5,21},{6,14},{7,23},{8,0},{9,25... | collective-permute-start | bytes 798728 | tf_op jit(solution)/shard_map/ppermute | solution.py:189
  4.2 11.0 %collective-permute-start.6 = (bf16[1040,128]{1,0:T(8,128)(2,1)S(1)}, bf16[1040,128]{1,0:T(8,128)(2,1)S(1)}, u32[]{:S(2)}, u32[]{:S(2)}) collective-permute-start(bf16[1040,128]{1,0:T(8,128)(2,1)S(1)} %collective-permute-done.4.refs_1_), channel_id=1, source_target_pairs={{0,8},{1,17},{2,10},{3,19},{4,12},{5,21},{6,14},{7,23},{8,0},{9,25... | collective-permute-start | bytes 798728 | tf_op jit(solution)/shard_map/ppermute | solution.py:189
  8.6 9.2 %collective-permute-start.1 = (bf16[1040,128]{1,0:T(8,128)(2,1)S(1)}, bf16[1040,128]{1,0:T(8,128)(2,1)S(1)}, u32[]{:S(2)}, u32[]{:S(2)}) collective-permute-start(bf16[1040,128]{1,0:T(8,128)(2,1)S(1)} %collective-permute-done.refs_2_), channel_id=1, source_target_pairs={{0,16},{1,9},{2,18},{3,11},{4,20},{5,13},{6,22},{7,15},{8,24},{9,1... | collective-permute-start | bytes 798728 | tf_op jit(solution)/shard_map/ppermute | solution.py:189
  10.7 9.7 %collective-permute-start.3 = (bf16[1040,128]{1,0:T(8,128)(2,1)S(1)}, bf16[1040,128]{1,0:T(8,128)(2,1)S(1)}, u32[]{:S(2)}, u32[]{:S(2)}) collective-permute-start(bf16[1040,128]{1,0:T(8,128)(2,1)S(1)} %prepare.1.refs_0_.refs_6_.refs_1_), channel_id=1, source_target_pairs={{0,4},{6,2},{1,3},{3,5},{5,7},{7,1},{8,12},{14,10},{9,11},{11,13},... | collective-permute-start | bytes 798728 | tf_op jit(solution)/shard_map/ppermute | solution.py:189
  15.2 5.2 %collective-permute-start.7 = (bf16[1040,128]{1,0:T(8,128)(2,1)S(1)}, bf16[1040,128]{1,0:T(8,128)(2,1)S(1)}, u32[]{:S(2)}, u32[]{:S(2)}) collective-permute-start(bf16[1040,128]{1,0:T(8,128)(2,1)S(1)} %collective-permute-done.refs_2_), channel_id=1, source_target_pairs={{0,1},{1,0},{2,3},{3,2},{4,5},{5,4},{6,7},{7,6},{8,9},{9,8},{10,11... | collective-permute-start | bytes 798728 | tf_op jit(solution)/shard_map/ppermute | solution.py:189
  15.3 5.1 %collective-permute-start.8 = (bf16[1040,128]{1,0:T(8,128)(2,1)S(1)}, bf16[1040,128]{1,0:T(8,128)(2,1)S(1)}, u32[]{:S(2)}, u32[]{:S(2)}) collective-permute-start(bf16[1040,128]{1,0:T(8,128)(2,1)S(1)} %collective-permute-done.6.refs_3_), channel_id=1, source_target_pairs={{0,1},{1,0},{2,3},{3,2},{4,5},{5,4},{6,7},{7,6},{8,9},{9,8},{10,11... | collective-permute-start | bytes 798728 | tf_op jit(solution)/shard_map/ppermute | solution.py:189
  15.8 9.2 %collective-permute-start.5 = (bf16[1040,128]{1,0:T(8,128)(2,1)S(1)}, bf16[1040,128]{1,0:T(8,128)(2,1)S(1)}, u32[]{:S(2)}, u32[]{:S(2)}) collective-permute-start(bf16[1040,128]{1,0:T(8,128)(2,1)S(1)} %collective-permute-done.4.refs_1_), channel_id=1, source_target_pairs={{0,4},{6,2},{1,3},{3,5},{5,7},{7,1},{8,12},{14,10},{9,11},{11,13},... | collective-permute-start | bytes 798728 | tf_op jit(solution)/shard_map/ppermute | solution.py:189
  17.8 8.0 %collective-permute-start.2 = (bf16[1040,128]{1,0:T(8,128)(2,1)S(1)}, bf16[1040,128]{1,0:T(8,128)(2,1)S(1)}, u32[]{:S(2)}, u32[]{:S(2)}) collective-permute-start(bf16[1040,128]{1,0:T(8,128)(2,1)S(1)} %collective-permute-done.1.refs_0_.refs_6_), channel_id=1, source_target_pairs={{0,1},{1,0},{2,3},{3,2},{4,5},{5,4},{6,7},{7,6},{8,9},{9,8},{10,11... | collective-permute-start | bytes 798728 | tf_op jit(solution)/shard_map/ppermute | solution.py:189

commit v4 on v3

--- a/solution.py
+++ b/solution.py
@@ -73,8 +73,8 @@
     mem = lax.axis_index("mem")
     core = mem % 2
     chip = mem // 2
-    near = grp ^ (1 + core)
-    other_near = grp ^ (2 - core)
+    near = grp ^ (2 - core)
+    other_near = grp ^ (1 + core)
     far = grp ^ 3
     row = chip * 2
     queries = [
@@ -87,13 +87,22 @@
         far * members + row + core,
         far * members + row + 1 - core,
     ]
-    keys = [None]
+    keys = [None, None]
     for pair in pairs:
-        source = jnp.int32(-1)
-        for side, table in enumerate(pair):
-            for origin, target in table:
-                source = jnp.where((core == side) & (chip == target), origin, source)
-        for sender in (core, 1 - core):
+        sources = []
+        for mine in (core, 1 - core):
+            source = jnp.int32(-1)
+            for side, table in enumerate(pair):
+                for origin, target in table:
+                    source = jnp.where(
+                        (mine == side) & (chip == target), origin, source
+                    )
+            sources.append(source)
+        for source, sender in (
+            (sources[0], core),
+            (sources[1], 1 - core),
+            (sources[0], 1 - core),
+        ):
             keys.append(jnp.where(source < 0, -1, grp * members + source * 2 + sender))
     return queries, keys
 
@@ -210,13 +219,16 @@
     slots += [[]] * (len(slots) % 2)
     pairs = [slots[i : i + 2] for i in range(0, len(slots), 2)]
     partner = swap(block)
-    near = send(block, across((1, 2)))
-    near_partner = send(partner, across((1, 2)))
-    far = send(near, across((2, 1)))
-    keys = [block]
+    near = send(block, across((2, 1)))
+    near_partner = send(partner, across((2, 1)))
+    far = send(near, across((1, 2)))
+    keys = [block, partner]
+    lines = []
     for pair in pairs:
-        keys.append(send(block, along(pair)))
+        line = send(block, along(pair))
+        keys += [line, swap(line)]
         keys.append(send(partner, along(pair)))
+        lines += [len(keys) - 3, len(keys) - 1]
     queries = [
         block,
         partner,
@@ -255,13 +267,13 @@
             ),
         )(*operands)
 
-    last = len(keys) - 1
     near_queries = list(range(QUERIES - 2))
-    first = list(range(last))
-    found = maxima([(near_queries, first)], None)
-    found = maxima([([QUERIES - 2], first)], found)
-    found = maxima([(list(range(QUERIES - 1)), [last])], found)
-    found = maxima([([QUERIES - 1], first + [last])], found)
+    far_query, swapped_query = QUERIES - 2, QUERIES - 1
+    shared = [0, 1, lines[0], lines[0] + 1]
+    found = maxima([(near_queries, [0] + lines[:-1])], None)
+    found = maxima([([far_query], shared + lines[1:-1])], found)
+    found = maxima([(near_queries + [far_query], lines[-1:])], found)
+    found = maxima([([swapped_query], lines[1:])], found)
     home = lax.all_to_all(
         found, ("grp", "mem"), split_axis=0, concat_axis=0, tiled=True
     )

time: 38.8 us -> 40 us (1.031)
  starting transfers between devices: 13.8 us -> 16.6 us
  waiting for transfers between devices: 8.87 us -> 7.21 us
    ppermute x9 -> x10, starting transfers between devices: 13.8 us -> 16.6 us  [send(): return lax.ppermute(value, ('grp', 'mem'), route)]
    ppermute x9 -> x10, waiting for transfers between devices: 8.87 us -> 7.21 us  [send(): return lax.ppermute(value, ('grp', 'mem'), route)]
  transfers between devices with their start and end apart: 9 -> 10, of which waited for: 3 -> 2; matrix products, arithmetic and copies ran while one was open for 0% -> 0% of each run, Pallas kernels for 5% -> 5%
where the time goes in v4:
time: 40 us; the launch traced here: 39.8 us
  starting transfers between devices  16.6 us (42%)
  blocking collectives  11.7 us (29%)
  waiting for transfers between devices  7.21 us (18%)
  Pallas kernels  3.57 us (9%)
  other arithmetic  0.56 us (1%)
    ppermute x10, starting transfers between devices, send(): return lax.ppermute(value, ('grp', 'mem'), route)  16.6 us
    all_to_all x1, blocking collectives, body(): lax.all_to_all(found, ('grp', 'mem'), split_axis=0, concat_axis=0, tiled=...  11.7 us
    ppermute x10, waiting for transfers between devices, send(): return lax.ppermute(value, ('grp', 'mem'), route)  7.21 us
    pallas_call x4, Pallas kernels, maxima(): pl.pallas_call(functools.partial(similarity_kernel, work, used_queries, u...  2.45 us
    pallas_call x1, Pallas kernels, body(): pl.pallas_call(prepare_kernel, out_shape=jax.ShapeDtypeStruct((width + ME...  1.12 us
  transfers between devices with their start and end apart: 10, of which 2 were waited for; matrix products, arithmetic and copies ran while one was open for 0% of the time, Pallas kernels for 5%

profile of v4, /device:TPU:0, one launch (start us, length us, event | category | flops | bytes accessed | tf_op | source)
XLA Modules:
  0.0 39.8 jit_solution(17911493319350755788)
XLA Ops:
  0.0 1.1 %prepare.1.refs_0_.refs_6_.refs_1_ = bf16[1040,128]{1,0:T(8,128)(2,1)S(1)} custom-call(bf16[128,1024]{1,0:T(8,128)(2,1)} %x_ref.1, s32[1,128]{1,0:T(1,128)} %bitcast.6, s32[1,128]{1,0:T(1,128)} %bitcast.7), custom_call_target="tpu_custom_call" | custom-call | tf_op jit(solution)/shard_map/prepare/pallas_call | solution.py:180
  1.1 0.6 %collective-permute-start.3 = (bf16[1040,128]{1,0:T(8,128)(2,1)S(1)}, bf16[1040,128]{1,0:T(8,128)(2,1)S(1)}, u32[]{:S(2)}, u32[]{:S(2)}) collective-permute-start(bf16[1040,128]{1,0:T(8,128)(2,1)S(1)} %prepare.1.refs_0_.refs_6_.refs_1_), channel_id=1, source_target_pairs={{0,1},{1,0},{2,3},{3,2},{4,5},{5,4},{6,7},{7,6},{8,9},{9,8},{10,11... | collective-permute-start | bytes 798728 | tf_op jit(solution)/shard_map/ppermute | solution.py:198
  1.7 2.6 %collective-permute-start = (bf16[1040,128]{1,0:T(8,128)(2,1)S(1)}, bf16[1040,128]{1,0:T(8,128)(2,1)S(1)}, u32[]{:S(2)}, u32[]{:S(2)}) collective-permute-start(bf16[1040,128]{1,0:T(8,128)(2,1)S(1)} %prepare.1.refs_0_.refs_6_.refs_1_), channel_id=1, source_target_pairs={{0,16},{1,9},{2,18},{3,11},{4,20},{5,13},{6,22},{7,15},{8,24},{9,1... | collective-permute-start | bytes 798728 | tf_op jit(solution)/shard_map/ppermute | solution.py:198
  4.3 0.0 collective-permute-done.3.refs_1_.refs_2_
  4.3 1.5 %collective-permute-start.5 = (bf16[1040,128]{1,0:T(8,128)(2,1)S(1)}, bf16[1040,128]{1,0:T(8,128)(2,1)S(1)}, u32[]{:S(2)}, u32[]{:S(2)}) collective-permute-start(bf16[1040,128]{1,0:T(8,128)(2,1)S(1)} %collective-permute-done.3.refs_1_.refs_2_), channel_id=1, source_target_pairs={{0,16},{1,9},{2,18},{3,11},{4,20},{5,13},{6,22},{7,15},{8,24},{9,1... | collective-permute-start | bytes 798728 | tf_op jit(solution)/shard_map/ppermute | solution.py:198
  5.7 4.5 %collective-permute-start.8 = (bf16[1040,128]{1,0:T(8,128)(2,1)S(1)}, bf16[1040,128]{1,0:T(8,128)(2,1)S(1)}, u32[]{:S(2)}, u32[]{:S(2)}) collective-permute-start(bf16[1040,128]{1,0:T(8,128)(2,1)S(1)} %prepare.1.refs_0_.refs_6_.refs_1_), channel_id=1, source_target_pairs={{0,4},{6,2},{1,3},{3,5},{5,7},{7,1},{8,12},{14,10},{9,11},{11,13},... | collective-permute-start | bytes 798728 | tf_op jit(solution)/shard_map/ppermute | solution.py:198
  10.2 0.0 collective-permute-done.refs_2_
  10.2 1.6 %collective-permute-start.1 = (bf16[1040,128]{1,0:T(8,128)(2,1)S(1)}, bf16[1040,128]{1,0:T(8,128)(2,1)S(1)}, u32[]{:S(2)}, u32[]{:S(2)}) collective-permute-start(bf16[1040,128]{1,0:T(8,128)(2,1)S(1)} %collective-permute-done.refs_2_), channel_id=1, source_target_pairs={{0,8},{1,17},{2,10},{3,19},{4,12},{5,21},{6,14},{7,23},{8,0},{9,25... | collective-permute-start | bytes 798728 | tf_op jit(solution)/shard_map/ppermute | solution.py:198
  11.8 0.0 collective-permute-start.6
  11.8 0.0 collective-permute-done.5.refs_3_
  11.8 0.5 %collective-permute-start.7 = (bf16[1040,128]{1,0:T(8,128)(2,1)S(1)}, bf16[1040,128]{1,0:T(8,128)(2,1)S(1)}, u32[]{:S(2)}, u32[]{:S(2)}) collective-permute-start(bf16[1040,128]{1,0:T(8,128)(2,1)S(1)} %collective-permute-done.5.refs_3_), channel_id=1, source_target_pairs={{0,1},{1,0},{2,3},{3,2},{4,5},{5,4},{6,7},{7,6},{8,9},{9,8},{10,11... | collective-permute-start | bytes 798728 | tf_op jit(solution)/shard_map/ppermute | solution.py:198
  12.3 2.6 %collective-permute-done.8.refs_7_.refs_3_ = bf16[1040,128]{1,0:T(8,128)(2,1)S(1)} collective-permute-done((bf16[1040,128]{1,0:T(8,128)(2,1)S(1)}, bf16[1040,128]{1,0:T(8,128)(2,1)S(1)}, u32[]{:S(2)}, u32[]{:S(2)}) %collective-permute-start.8) | collective-permute-done | bytes 266272 | tf_op jit(solution)/shard_map/ppermute | solution.py:198
  14.9 1.4 %collective-permute-start.9 = (bf16[1040,128]{1,0:T(8,128)(2,1)S(1)}, bf16[1040,128]{1,0:T(8,128)(2,1)S(1)}, u32[]{:S(2)}, u32[]{:S(2)}) collective-permute-start(bf16[1040,128]{1,0:T(8,128)(2,1)S(1)} %collective-permute-done.8.refs_7_.refs_3_), channel_id=1, source_target_pairs={{0,1},{1,0},{2,3},{3,2},{4,5},{5,4},{6,7},{7,6},{8,9},{9,8},{10,11... | collective-permute-start | bytes 798728 | tf_op jit(solution)/shard_map/ppermute | solution.py:198
  16.2 4.0 %collective-permute-start.4 = (bf16[1040,128]{1,0:T(8,128)(2,1)S(1)}, bf16[1040,128]{1,0:T(8,128)(2,1)S(1)}, u32[]{:S(2)}, u32[]{:S(2)}) collective-permute-start(bf16[1040,128]{1,0:T(8,128)(2,1)S(1)} %collective-permute-done.3.refs_1_.refs_2_), channel_id=1, source_target_pairs={{0,4},{6,2},{1,3},{3,5},{5,7},{7,1},{8,12},{14,10},{9,11},{11,13},... | collective-permute-start | bytes 798728 | tf_op jit(solution)/shard_map/ppermute | solution.py:198
  20.3 0.0 collective-permute-done.1.refs_0_.refs_6_
  20.3 0.1 collective-permute-start.2
  20.4 0.0 collective-permute-done.6.refs_4_
  20.4 0.0 collective-permute-done.7.refs_5_
  20.4 0.7 %shard_map.37.refs_5_ = f32[32,128]{1,0:T(8,128)S(1)} custom-call(bf16[1040,128]{1,0:T(8,128)(2,1)S(1)} %prepare.1.refs_0_.refs_6_.refs_1_, bf16[1040,128]{1,0:T(8,128)(2,1)S(1)} %collective-permute-done.3.refs_1_.refs_2_, bf16[1040,128]{1,0:T(8,128)(2,1)S(1)} %collective-permute-done.refs_2_, bf16[1040,128]{1,0:T(8,128)(2,1)S(1)} %collective-permute-done.5.refs_3_, ...), custom_call_target="tpu_custom_call" | custom-call | flops 402653184 | tf_op jit(solution)/shard_map/pallas_call | solution.py:249
  21.2 0.0 collective-permute-done.9.refs_4_
  21.2 0.6 %shard_map.38.refs_8_ = f32[32,128]{1,0:T(8,128)S(1)} custom-call(bf16[1040,128]{1,0:T(8,128)(2,1)S(1)} %collective-permute-done.1.refs_0_.refs_6_, bf16[1040,128]{1,0:T(8,128)(2,1)S(1)} %prepare.1.refs_0_.refs_6_.refs_1_, bf16[1040,128]{1,0:T(8,128)(2,1)S(1)} %collective-permute-done.3.refs_1_.refs_2_, ...), custom_call_target="tpu_custom_call" | custom-call | flops 134217728 | tf_op jit(solution)/shard_map/pallas_call | solution.py:249
  21.8 4.6 %collective-permute-done.4.refs_7_.refs_1_ = bf16[1040,128]{1,0:T(8,128)(2,1)S(1)} collective-permute-done((bf16[1040,128]{1,0:T(8,128)(2,1)S(1)}, bf16[1040,128]{1,0:T(8,128)(2,1)S(1)}, u32[]{:S(2)}, u32[]{:S(2)}) %collective-permute-start.4) | collective-permute-done | bytes 266272 | tf_op jit(solution)/shard_map/ppermute | solution.py:198
  26.4 0.8 %shard_map.39.refs_2_ = f32[32,128]{1,0:T(8,128)S(1)} custom-call(bf16[1040,128]{1,0:T(8,128)(2,1)S(1)} %prepare.1.refs_0_.refs_6_.refs_1_, bf16[1040,128]{1,0:T(8,128)(2,1)S(1)} %collective-permute-done.3.refs_1_.refs_2_, bf16[1040,128]{1,0:T(8,128)(2,1)S(1)} %collective-permute-done.refs_2_, bf16[1040,128]{1,0:T(8,128)(2,1)S(1)} %collective-permute-done.5.refs_3_, ...), custom_call_target="tpu_custom_call" | custom-call | flops 234881024 | tf_op jit(solution)/shard_map/pallas_call | solution.py:249
  27.2 0.0 collective-permute-done.2.refs_0_
  27.2 0.3 shard_map.40
  27.5 11.7 %all_to_all.9 = f32[32,1,128]{2,1,0:T(1,128)S(1)} all-to-all(f32[32,1,128]{2,1,0:T(1,128)S(1)} %bitcast.5), channel_id=1, replica_groups=mesh['grp'=4,'mem'=8] {'grp','mem'}, dimensions={0} | all-to-all | bytes 32768 | tf_op jit(solution)/shard_map/all_to_all | solution.py:277
  39.2 0.6 %reduce_max.9 = f32[128]{0:T(128)} reduce(f32[32,1,128]{2,1,0:T(1,128)S(1)} %all_to_all.9, f32[]{:T(128)} %constant.0.clone.1), dimensions={0,1}, to_apply=%region_0.0 | reduce | flops 3968 | bytes 16900 | tf_op jit(solution)/shard_map/reduce_max | solution.py:280
Async XLA Ops:
  1.1 3.1 %collective-permute-start.3 = (bf16[1040,128]{1,0:T(8,128)(2,1)S(1)}, bf16[1040,128]{1,0:T(8,128)(2,1)S(1)}, u32[]{:S(2)}, u32[]{:S(2)}) collective-permute-start(bf16[1040,128]{1,0:T(8,128)(2,1)S(1)} %prepare.1.refs_0_.refs_6_.refs_1_), channel_id=1, source_target_pairs={{0,1},{1,0},{2,3},{3,2},{4,5},{5,4},{6,7},{7,6},{8,9},{9,8},{10,11... | collective-permute-start | bytes 798728 | tf_op jit(solution)/shard_map/ppermute | solution.py:198
  1.7 8.6 %collective-permute-start = (bf16[1040,128]{1,0:T(8,128)(2,1)S(1)}, bf16[1040,128]{1,0:T(8,128)(2,1)S(1)}, u32[]{:S(2)}, u32[]{:S(2)}) collective-permute-start(bf16[1040,128]{1,0:T(8,128)(2,1)S(1)} %prepare.1.refs_0_.refs_6_.refs_1_), channel_id=1, source_target_pairs={{0,16},{1,9},{2,18},{3,11},{4,20},{5,13},{6,22},{7,15},{8,24},{9,1... | collective-permute-start | bytes 798728 | tf_op jit(solution)/shard_map/ppermute | solution.py:198
  4.3 7.5 %collective-permute-start.5 = (bf16[1040,128]{1,0:T(8,128)(2,1)S(1)}, bf16[1040,128]{1,0:T(8,128)(2,1)S(1)}, u32[]{:S(2)}, u32[]{:S(2)}) collective-permute-start(bf16[1040,128]{1,0:T(8,128)(2,1)S(1)} %collective-permute-done.3.refs_1_.refs_2_), channel_id=1, source_target_pairs={{0,16},{1,9},{2,18},{3,11},{4,20},{5,13},{6,22},{7,15},{8,24},{9,1... | collective-permute-start | bytes 798728 | tf_op jit(solution)/shard_map/ppermute | solution.py:198
  5.7 9.2 %collective-permute-start.8 = (bf16[1040,128]{1,0:T(8,128)(2,1)S(1)}, bf16[1040,128]{1,0:T(8,128)(2,1)S(1)}, u32[]{:S(2)}, u32[]{:S(2)}) collective-permute-start(bf16[1040,128]{1,0:T(8,128)(2,1)S(1)} %prepare.1.refs_0_.refs_6_.refs_1_), channel_id=1, source_target_pairs={{0,4},{6,2},{1,3},{3,5},{5,7},{7,1},{8,12},{14,10},{9,11},{11,13},... | collective-permute-start | bytes 798728 | tf_op jit(solution)/shard_map/ppermute | solution.py:198
  10.2 10.1 %collective-permute-start.1 = (bf16[1040,128]{1,0:T(8,128)(2,1)S(1)}, bf16[1040,128]{1,0:T(8,128)(2,1)S(1)}, u32[]{:S(2)}, u32[]{:S(2)}) collective-permute-start(bf16[1040,128]{1,0:T(8,128)(2,1)S(1)} %collective-permute-done.refs_2_), channel_id=1, source_target_pairs={{0,8},{1,17},{2,10},{3,19},{4,12},{5,21},{6,14},{7,23},{8,0},{9,25... | collective-permute-start | bytes 798728 | tf_op jit(solution)/shard_map/ppermute | solution.py:198
  11.8 8.6 %collective-permute-start.6 = (bf16[1040,128]{1,0:T(8,128)(2,1)S(1)}, bf16[1040,128]{1,0:T(8,128)(2,1)S(1)}, u32[]{:S(2)}, u32[]{:S(2)}) collective-permute-start(bf16[1040,128]{1,0:T(8,128)(2,1)S(1)} %collective-permute-done.refs_2_), channel_id=1, source_target_pairs={{0,1},{1,0},{2,3},{3,2},{4,5},{5,4},{6,7},{7,6},{8,9},{9,8},{10,11... | collective-permute-start | bytes 798728 | tf_op jit(solution)/shard_map/ppermute | solution.py:198
  11.8 8.6 %collective-permute-start.7 = (bf16[1040,128]{1,0:T(8,128)(2,1)S(1)}, bf16[1040,128]{1,0:T(8,128)(2,1)S(1)}, u32[]{:S(2)}, u32[]{:S(2)}) collective-permute-start(bf16[1040,128]{1,0:T(8,128)(2,1)S(1)} %collective-permute-done.5.refs_3_), channel_id=1, source_target_pairs={{0,1},{1,0},{2,3},{3,2},{4,5},{5,4},{6,7},{7,6},{8,9},{9,8},{10,11... | collective-permute-start | bytes 798728 | tf_op jit(solution)/shard_map/ppermute | solution.py:198
  14.9 6.3 %collective-permute-start.9 = (bf16[1040,128]{1,0:T(8,128)(2,1)S(1)}, bf16[1040,128]{1,0:T(8,128)(2,1)S(1)}, u32[]{:S(2)}, u32[]{:S(2)}) collective-permute-start(bf16[1040,128]{1,0:T(8,128)(2,1)S(1)} %collective-permute-done.8.refs_7_.refs_3_), channel_id=1, source_target_pairs={{0,1},{1,0},{2,3},{3,2},{4,5},{5,4},{6,7},{7,6},{8,9},{9,8},{10,11... | collective-permute-start | bytes 798728 | tf_op jit(solution)/shard_map/ppermute | solution.py:198
  16.2 10.1 %collective-permute-start.4 = (bf16[1040,128]{1,0:T(8,128)(2,1)S(1)}, bf16[1040,128]{1,0:T(8,128)(2,1)S(1)}, u32[]{:S(2)}, u32[]{:S(2)}) collective-permute-start(bf16[1040,128]{1,0:T(8,128)(2,1)S(1)} %collective-permute-done.3.refs_1_.refs_2_), channel_id=1, source_target_pairs={{0,4},{6,2},{1,3},{3,5},{5,7},{7,1},{8,12},{14,10},{9,11},{11,13},... | collective-permute-start | bytes 798728 | tf_op jit(solution)/shard_map/ppermute | solution.py:198
  20.3 6.9 %collective-permute-start.2 = (bf16[1040,128]{1,0:T(8,128)(2,1)S(1)}, bf16[1040,128]{1,0:T(8,128)(2,1)S(1)}, u32[]{:S(2)}, u32[]{:S(2)}) collective-permute-start(bf16[1040,128]{1,0:T(8,128)(2,1)S(1)} %collective-permute-done.1.refs_0_.refs_6_), channel_id=1, source_target_pairs={{0,1},{1,0},{2,3},{3,2},{4,5},{5,4},{6,7},{7,6},{8,9},{9,8},{10,11... | collective-permute-start | bytes 798728 | tf_op jit(solution)/shard_map/ppermute | solution.py:198
